TPU v7x, 32 devices: a whole 2x2x4 slice. The times are simulated.
32 devices in a mesh: row: 8 (over y, x, core), col: 4 (over z).
Axes of the slice: x: 2, y: 2, z: 4, core: 2. Of those that a mesh axis runs over, the one named last changes fastest.
Arguments:
- right_side: float32 [2, 2048, 1024], P(None, 'row', 'col'), may hold values from -6 to 6
- probe: float32 [2, 256, 256], replicated, may hold values from -6 to 6
- detector_weights: float32 [256, 256], replicated, may hold values from 0.1 to 10
- offsets: int32 [8, 4, 4, 2], P('row', 'col'), may hold values from -128 to 127, as said below
- counts: int32 [8, 4], P('row', 'col'), may hold values from 2 to 4, as said below
Outputs:
- solution_field: float32 [2, 2048, 1024], P(None, 'row', 'col')
- residual: float32 [2, 2048, 1024], P(None, 'row', 'col')
Inputs may be any that keep to these rules, and one draw needn't show every extreme that they name: `counts`: every region holds at least two positions; in every draw some region holds exactly 4. In every region slot 0 has both offsets negative and slot 1 both offsets non-negative.
All inputs are finite; a program needn't handle non-finite values.
Results may differ from a plain program's by a relative error of at most 0.0003.
Values sent between devices are 32-bit elements; how exact they have to be, the bound alone decides.
No kernel may reach another device: no remote copies, remote signals or barrier semaphores. Data moves between devices by JAX's collectives and lax.ppermute only.
A program may use at most 64 MiB of HBM per device.

v0:
```python
import functools
import math

import jax
import jax.numpy as jnp
import numpy as np
from jax import lax
from jax.experimental import pallas as pl
from jax.experimental.pallas import tpu as pltpu
from jax.sharding import PartitionSpec as P

ITERS = 3
RIDGE = 0.5
CHUNK = 16
F32 = jnp.float32
BF16 = jnp.bfloat16
VMEM = pl.BlockSpec(memory_space=pltpu.VMEM)
SMEM = pl.BlockSpec(memory_space=pltpu.SMEM)


def pairs(axis, parity):
    count = lax.axis_size(axis)
    out = []
    for low in range(parity, count - 1, 2):
        out += [(low, low + 1), (low + 1, low)]
    return out


def swap(value, axis, parity):
    return lax.ppermute(value, axis, pairs(axis, parity))


def all_sum(value):
    for axis in ("row", "col"):
        count = lax.axis_size(axis)
        if count & (count - 1):
            value = lax.psum(value, axis)
            continue
        step = 1
        while step < count:
            value = value + lax.ppermute(value, axis, [(i, i ^ step) for i in range(count)])
            step *= 2
    return value


def split_np(mat):
    high = mat.astype(np.float32).astype(jnp.bfloat16)
    low = (mat - high.astype(np.float64)).astype(np.float32).astype(jnp.bfloat16)
    return high, low


def tables(length):
    half = length // 2
    spot = np.arange(half)
    lanes, rows = [], []
    for odd in (0, 1):
        phase = (spot[:, None] * (2 * spot[None, :] + odd)) % length
        angle = phase * (2.0 * math.pi / length)
        cos = np.cos(angle) / math.sqrt(length)
        sin = np.sin(angle) / math.sqrt(length)
        forward = np.block([[cos, -sin], [sin, cos]])
        for mat in (forward, forward.T):
            high, low = split_np(mat)
            lanes.append(np.concatenate([high, high, low], axis=0))
            high, low = split_np(mat.T)
            rows.append(np.concatenate([high, low, high], axis=1))
    return np.stack(lanes), np.stack(rows)


def split(value):
    high = value.astype(BF16)
    low = (value - high.astype(F32)).astype(BF16)
    return high, low


def dot(left, right):
    return jnp.dot(left, right, preferred_element_type=F32)


def total(ref):
    return jnp.sum(ref, keepdims=True)


def prep_kernel(side, cap, info, block, probe, zone_a, zone_b, rolled):
    half = side // 2
    par_r, par_c = info[0], info[1]
    for cz, out in ((0, zone_a), (1, zone_b)):
        right = (cz ^ 1 ^ par_c) == 1
        for rz in (0, 1):
            base = pl.multiple_of((rz ^ 1 ^ par_r) * half, half)
            for comp in (0, 1):
                rows = block[comp, pl.ds(base, half), :]
                out[rz, comp] = jnp.where(right, rows[:, half:], rows[:, :half])

    for slot in range(cap):
        row_by = lax.rem(info[5 + 2 * slot] + side, side)
        col_by = lax.rem(info[6 + 2 * slot] + side, side)
        for comp in (0, 1):
            moved = pltpu.roll(probe[comp], row_by, 0)
            rolled[slot, comp] = pltpu.roll(moved, col_by, 1)


def coefficients(stage, sums):
    norms = [total(s[0]) for s in sums]
    prods = [total(s[1]) for s in sums]
    alphas, ratios = [], []
    for k in range(stage):
        if k == 0:
            alphas.append(norms[0] / prods[0])
            ratios.append(None)
        else:
            ratio = norms[k] / norms[k - 1]
            ratios.append(ratio)
            alphas.append(norms[k] / (prods[k] - ratio * norms[k] / alphas[k - 1]))
    return alphas, ratios


def apply_kernel(side, cap, stage, *refs):
    half = side // 2
    n_sums = stage
    info, rolled, weights, lanes, rows = refs[:5]
    pos = 5
    sums = refs[pos : pos + n_sums]
    pos += n_sums
    window = refs[pos : pos + 4]
    pos += 4
    if stage >= 1:
        field_old = refs[pos]
        pos += 1
    if stage >= 2:
        along_old = refs[pos]
        pos += 1
    field = refs[pos]
    pos += 1
    if stage >= 1:
        along = refs[pos]
        pos += 1
    own_out = refs[pos : pos + 2]
    far_out = refs[pos + 2 : pos + 4]
    partial = refs[pos + 4]
    pos += 5
    lhs, mid, rhs, freq, terms = refs[pos : pos + 5]

    par_r, par_c, count = info[0], info[1], info[4]

    if stage == 0:
        for z in range(4):
            for b in range(8):
                idx = (b // 4, (b // 2) % 2, b % 2)
                field[(z,) + idx] = window[z][idx]
    else:
        alphas, ratios = coefficients(stage, sums)
        alpha, ratio = alphas[-1], ratios[-1]
        for z in range(4):
            for b in range(8):
                idx = (b // 4, (b // 2) % 2, b % 2)
                for q in range(0, half, 2 * CHUNK):
                    at = (z,) + idx + (slice(q, q + 2 * CHUNK),)
                    value = window[z][idx + (slice(q, q + 2 * CHUNK),)]
                    if stage >= 2:
                        value = value + ratio * along_old[at]
                    along[at] = value
                    field[at] = field_old[at] - alpha * value

    partial[...] = jnp.zeros_like(partial)

    @pl.when(count <= 2)
    def _():
        terms[2:] = jnp.zeros_like(terms[2:])

    row_iota = lax.broadcasted_iota(jnp.int32, (CHUNK, half), 0)
    col_iota = lax.broadcasted_iota(jnp.int32, (CHUNK, half), 1)

    def marks(slot):
        out = []
        for d in (0, 1):
            off = info[5 + 2 * slot + d]
            neg = off < 0
            out.append(jnp.where(neg, -1, 1))
            out.append(jnp.where(neg, 1 - (off + side), off))
        return out

    def visit(pair, carry):
        slots = (2 * pair, 2 * pair + 1)
        for j, slot in enumerate(slots):
            row_sign, row_from, col_sign, col_from = marks(slot)
            col_own = [(col_iota + l * half) * col_sign >= col_from for l in (0, 1)]
            for h in (0, 1):
                own_z = h ^ 1 ^ par_r
                far_z = 2 + (h ^ par_r)
                for q in range(0, half, CHUNK):
                    row_own = (row_iota + (h * half + q)) * row_sign >= row_from
                    cut = slice(q, q + CHUNK)
                    waves = []
                    for l in (0, 1):
                        own_c = l ^ 1 ^ par_c
                        far_c = l ^ par_c
                        got = []
                        for comp in (0, 1):
                            near = jnp.where(
                                col_own[l],
                                field[own_z, own_c, 0, comp, cut],
                                field[own_z, far_c, 1, comp, cut],
                            )
                            beyond = jnp.where(
                                col_own[l],
                                field[far_z, own_c, 0, comp, cut],
                                field[far_z, far_c, 1, comp, cut],
                            )
                            got.append(jnp.where(row_own, near, beyond))
                        at = (slice(h * half + q, h * half + q + CHUNK), slice(l * half, l * half + half))
                        p_re = rolled[(slot, 0) + at]
                        p_im = rolled[(slot, 1) + at]
                        waves.append((p_re * got[0] - p_im * got[1], p_re * got[1] + p_im * got[0]))
                    to = slice(j * side + h * half + q, j * side + h * half + q + CHUNK)
                    for comp in (0, 1):
                        a, b = waves[0][comp], waves[1][comp]
                        for odd, value in ((0, a + b), (1, a - b)):
                            high, low = split(value)
                            lo_at = comp * half
                            lhs[odd, to, lo_at : lo_at + half] = high
                            lhs[odd, to, side + lo_at : side + lo_at + half] = low
                            lhs[odd, to, 2 * side + lo_at : 2 * side + lo_at + half] = high

        for odd in (0, 1):
            mid[odd] = dot(lhs[odd], lanes[2 * odd])

        for j in (0, 1):
            for odd in (0, 1):
                for q in range(0, half, CHUNK):
                    top = mid[odd, j * side + q : j * side + q + CHUNK]
                    low_rows = mid[odd, j * side + half + q : j * side + half + q + CHUNK]
                    for which, value in ((0, top + low_rows), (1, top - low_rows)):
                        for comp in (0, 1):
                            high, low = split(value[:, comp * half : comp * half + half])
                            to = slice(j * side + odd * half, j * side + odd * half + half)
                            k = comp * half + q
                            rhs[which, k : k + CHUNK, to] = high
                            rhs[which, side + k : side + k + CHUNK, to] = high
                            rhs[which, 2 * side + k : 2 * side + k + CHUNK, to] = low

        for which in (0, 1):
            freq[which] = dot(rows[2 * which], rhs[which])

        for which in (0, 1):
            gathered = [jnp.zeros((8, half), F32), jnp.zeros((8, half), F32)]
            for j in (0, 1):
                for odd in (0, 1):
                    to = slice(j * side + odd * half, j * side + odd * half + half)
                    for comp in (0, 1):
                        for q in range(0, half, CHUNK):
                            value = freq[which, comp * half + q : comp * half + q + CHUNK, to]
                            scaled = value * weights[which, q : q + CHUNK, odd * half : odd * half + half]
                            both = value * scaled
                            for e in range(0, CHUNK, 8):
                                gathered[j] = gathered[j] + both[e : e + 8]
                            high, low = split(scaled)
                            k = comp * half + q
                            rhs[which, k : k + CHUNK, to] = high
                            rhs[which, side + k : side + k + CHUNK, to] = high
                            rhs[which, 2 * side + k : 2 * side + k + CHUNK, to] = low
            for j, slot in enumerate(slots):
                partial[1] += jnp.where(slot < count, gathered[j], 0.0)

        for which in (0, 1):
            freq[which] = dot(rows[2 * which + 1], rhs[which])

        for j in (0, 1):
            for odd in (0, 1):
                to = slice(j * side + odd * half, j * side + odd * half + half)
                for comp in (0, 1):
                    for q in range(0, half, CHUNK):
                        even_part = freq[0, comp * half + q : comp * half + q + CHUNK, to]
                        odd_part = freq[1, comp * half + q : comp * half + q + CHUNK, to]
                        for h, value in ((0, even_part + odd_part), (1, even_part - odd_part)):
                            high, low = split(value)
                            at = slice(j * side + h * half + q, j * side + h * half + q + CHUNK)
                            lo_at = comp * half
                            lhs[odd, at, lo_at : lo_at + half] = high
                            lhs[odd, at, side + lo_at : side + lo_at + half] = low
                            lhs[odd, at, 2 * side + lo_at : 2 * side + lo_at + half] = high

        for odd in (0, 1):
            mid[odd] = dot(lhs[odd], lanes[2 * odd + 1])

        for j, slot in enumerate(slots):
            used = slot < count
            for h in (0, 1):
                for q in range(0, half, CHUNK):
                    at = slice(j * side + h * half + q, j * side + h * half + q + CHUNK)
                    even_part, odd_part = mid[0, at], mid[1, at]
                    for l, value in ((0, even_part + odd_part), (1, even_part - odd_part)):
                        v_re, v_im = value[:, :half], value[:, half:]
                        spot = (slice(h * half + q, h * half + q + CHUNK), slice(l * half, l * half + half))
                        p_re = rolled[(slot, 0) + spot]
                        p_im = rolled[(slot, 1) + spot]
                        cut = slice(q, q + CHUNK)
                        terms[slot, h, l, 0, cut] = jnp.where(used, p_re * v_re + p_im * v_im, 0.0)
                        terms[slot, h, l, 1, cut] = jnp.where(used, p_re * v_im - p_im * v_re, 0.0)
        return carry

    lax.fori_loop(0, (count + 1) // 2, visit, 0)

    norm = jnp.zeros((8, half), F32)
    for rz in (0, 1):
        for rk, out in ((0, own_out[rz]), (1, far_out[rz])):
            h = (rz ^ par_r) if rk else (rz ^ 1 ^ par_r)
            for cz in (0, 1):
                for ck in (0, 1):
                    l = (cz ^ par_c) if ck else (cz ^ 1 ^ par_c)
                    col_masks, row_marks = [], []
                    for slot in range(cap):
                        row_sign, row_from, col_sign, col_from = marks(slot)
                        own = (col_iota + l * half) * col_sign >= col_from
                        col_masks.append(jnp.logical_not(own) if ck else own)
                        row_marks.append((row_sign, row_from))
                    for q in range(0, half, CHUNK):
                        cut = slice(q, q + CHUNK)
                        acc = [None, None]
                        if rk == 0 and ck == 0:
                            for comp in (0, 1):
                                value = field[rz, cz, 0, comp, cut]
                                acc[comp] = RIDGE * value
                                sq = value * value
                                for e in range(0, CHUNK, 8):
                                    norm = norm + sq[e : e + 8]
                        for slot in range(cap):
                            row_sign, row_from = row_marks[slot]
                            spots = (row_iota + (h * half + q)) * row_sign
                            mask = (spots < row_from) if rk else (spots >= row_from)
                            mask = jnp.logical_and(mask, col_masks[slot])
                            for comp in (0, 1):
                                value = jnp.where(mask, terms[slot, h, l, comp, cut], 0.0)
                                acc[comp] = value if acc[comp] is None else acc[comp] + value
                        for comp in (0, 1):
                            out[cz, ck, comp, cut] = acc[comp]
    partial[0] = norm
    partial[1] += RIDGE * norm


def final_kernel(side, stage, *refs):
    half = side // 2
    info = refs[0]
    sums = refs[1 : 1 + stage]
    fields = refs[1 + stage : 1 + 2 * stage]
    along_old = refs[1 + 2 * stage]
    mine = refs[2 + 2 * stage : 6 + 2 * stage]
    theirs = refs[6 + 2 * stage : 10 + 2 * stage]
    solved, left = refs[10 + 2 * stage :]
    par_r, par_c = info[0], info[1]
    alphas, ratios = coefficients(stage, sums)
    for rz in (0, 1):
        for cz in (0, 1):
            for comp in (0, 1):
                for q in range(0, half, 2 * CHUNK):
                    cut = slice(q, q + 2 * CHUNK)
                    image = mine[2 * rz + cz][0, comp, cut] + theirs[2 * rz + cz][comp, cut]
                    value = image + ratios[-1] * along_old[rz, cz, 0, comp, cut]
                    residual = fields[-1][rz, cz, 0, comp, cut]
                    direction = fields[0][rz, cz, 0, comp, cut]
                    answer = alphas[0] * direction
                    for k in range(1, stage):
                        direction = fields[k][rz, cz, 0, comp, cut] + ratios[k] * direction
                        answer = answer + alphas[k] * direction
                    residual = residual - alphas[-1] * value
                    at = pl.ds(pl.multiple_of((rz ^ 1 ^ par_r) * half + q, 2 * CHUNK), 2 * CHUNK)
                    for right in (0, 1):
                        @pl.when((cz ^ 1 ^ par_c) == right)
                        def _():
                            solved[comp, at, right * half : right * half + half] = answer
                            left[comp, at, right * half : right * half + half] = residual


def local(right_side, probe, detector_weights, offsets, counts):
    side = probe.shape[1]
    half = side // 2
    cap = offsets.shape[2]
    row_at, col_at = lax.axis_index("row"), lax.axis_index("col")
    row_n, col_n = lax.axis_size("row"), lax.axis_size("col")
    par_r, par_c = row_at % 2, col_at % 2

    def partner(at, par, count, zone):
        other = at + (1 - 2 * (par ^ zone))
        return jnp.logical_and(other >= 0, other < count)

    near_col = [partner(col_at, par_c, col_n, z).astype(F32) for z in (0, 1)]
    info = jnp.concatenate(
        [
            jnp.stack([par_r, par_c, par_r, par_c, counts[0, 0]]).astype(jnp.int32),
            offsets.reshape(-1).astype(jnp.int32),
        ]
    )
    lanes, rows = tables(side)
    lanes, rows = jnp.asarray(lanes), jnp.asarray(rows)
    weights = (
        detector_weights.reshape(half, 2, half, 2).transpose(1, 0, 3, 2).reshape(2, half, side)
    )

    zone = jax.ShapeDtypeStruct((2, 2, half, half), F32)
    strip = jax.ShapeDtypeStruct((2, 2, 2, half, half), F32)
    whole = jax.ShapeDtypeStruct((4, 2, 2, 2, half, half), F32)
    tiny = jax.ShapeDtypeStruct((2, 8, half), F32)

    zone_a, zone_b, rolled = pl.pallas_call(
        functools.partial(prep_kernel, side, cap),
        out_shape=(zone, zone, jax.ShapeDtypeStruct((cap, 2, side, side), F32)),
        in_specs=[SMEM, VMEM, VMEM],
        out_specs=(VMEM, VMEM, VMEM),
        compiler_params=pltpu.CompilerParams(vmem_limit_bytes=16 * 2**20),
    )(info, right_side, probe)

    def apply_op(stage, sums, window, field_old, along_old):
        args = [info, rolled, weights, lanes, rows, *sums, *window]
        outs = [whole]
        if stage >= 1:
            args.append(field_old)
            outs.append(whole)
        if stage >= 2:
            args.append(along_old)
        outs += [strip] * 4 + [tiny]
        got = pl.pallas_call(
            functools.partial(apply_kernel, side, cap, stage),
            out_shape=tuple(outs),
            in_specs=[SMEM] + [VMEM] * (len(args) - 1),
            out_specs=tuple([VMEM] * len(outs)),
            scratch_shapes=[
                pltpu.VMEM((2, 2 * side, 3 * side), BF16),
                pltpu.VMEM((2, 2 * side, side), F32),
                pltpu.VMEM((2, 3 * side, 2 * side), BF16),
                pltpu.VMEM((2, side, 2 * side), F32),
                pltpu.VMEM((cap, 2, 2, 2, half, half), F32),
            ],
            compiler_params=pltpu.CompilerParams(vmem_limit_bytes=32 * 2**20),
        )(*args)
        field = got[0]
        along = got[1] if stage >= 1 else None
        rest = got[2:] if stage >= 1 else got[1:]
        return field, along, rest[0:2], rest[2:4], rest[4]

    zones = (zone_a, zone_b)
    beyond = [swap(zones[z], "col", z) for z in (0, 1)]
    near = [
        jnp.stack([jnp.stack([zones[cz][rz], beyond[cz][rz]]) for cz in (0, 1)]) for rz in (0, 1)
    ]
    far = [swap(near[z], "row", z) for z in (0, 1)]
    window = (near[0], near[1], far[0], far[1])

    sums, fields = [], []
    field = along = None
    for stage in range(ITERS):
        field, along_new, own, sent, partial = apply_op(stage, sums, window, field, along)
        fields.append(field)
        along = along_new
        reduced = [own[z] + swap(sent[z], "row", z) for z in (0, 1)]
        sums = sums + [all_sum(partial)]
        mine = [reduced[rz][cz] for rz in (0, 1) for cz in (0, 1)]
        if stage + 1 < ITERS:
            got = [swap(mine[2 * rz + cz], "col", cz) for rz in (0, 1) for cz in (0, 1)]
            near = []
            for rz in (0, 1):
                parts = []
                for cz in (0, 1):
                    m, g = mine[2 * rz + cz], got[2 * rz + cz]
                    parts.append(jnp.stack([m[0] + g[1], (m[1] + g[0]) * near_col[cz]]))
                near.append(jnp.stack(parts))
            far = [swap(near[z], "row", z) for z in (0, 1)]
            window = (near[0], near[1], far[0], far[1])
        else:
            got = [swap(mine[2 * rz + cz][1], "col", cz) for rz in (0, 1) for cz in (0, 1)]

    out = jax.ShapeDtypeStruct(right_side.shape, F32)
    args = [info, *sums, *fields, along, *mine, *got]
    return pl.pallas_call(
        functools.partial(final_kernel, side, ITERS),
        out_shape=(out, out),
        in_specs=[SMEM] + [VMEM] * (len(args) - 1),
        out_specs=(VMEM, VMEM),
        compiler_params=pltpu.CompilerParams(vmem_limit_bytes=16 * 2**20),
    )(*args)


def solution(mesh):
    placed = (P(None, "row", "col"), P(), P(), P("row", "col", None, None), P("row", "col"))
    return jax.shard_map(
        local,
        mesh=mesh,
        in_specs=placed,
        out_specs=(P(None, "row", "col"), P(None, "row", "col")),
        check_vma=False,
    )
```

profile of v0, /device:TPU:0, one launch (start us, length us, event | category | flops | bytes accessed | tf_op | source)
XLA Modules:
  0.0 219.7 jit_solution(10039556021588908447)
XLA Ops:
  6.3 5.9 %collective-permute-start = (f32[2,2,128,128]{3,2,1,0:T(8,128)S(1)}, f32[2,2,128,128]{3,2,1,0:T(8,128)S(1)}, u32[]{:S(2)}, u32[]{:S(2)}) collective-permute-start(f32[2,2,128,128]{3,2,1,0:T(8,128)S(1)} %get-tuple-element.26), channel_id=1, source_target_pairs={{0,1},{1,0},{2,3},{3,2},{4,5},{5,4},{6,7},{7,6},{8,9},{9,8},{10,11... | collective-permute-start | bytes 786440 | tf_op jit(solution)/shard_map/ppermute | solution.py:30
  12.3 5.9 %collective-permute-done = f32[2,2,128,128]{3,2,1,0:T(8,128)S(1)} collective-permute-done((f32[2,2,128,128]{3,2,1,0:T(8,128)S(1)}, f32[2,2,128,128]{3,2,1,0:T(8,128)S(1)}, u32[]{:S(2)}, u32[]{:S(2)}) %collective-permute-start) | collective-permute-done | bytes 262176 | tf_op jit(solution)/shard_map/ppermute | solution.py:30
  20.0 18.8 %reshape.70 = f32[128,2,128,2]{3,2,1,0:T(8,128)} reshape(f32[256,256]{1,0:T(8,128)} %param.9) | data formatting | bytes 524288 | tf_op jit(solution)/shard_map/reshape | solution.py:396
  38.8 9.8 %copy.12 = f32[2,128,2,128]{3,2,1,0:T(2,128)} copy(f32[2,128,2,128]{2,3,0,1:T(8,128)} %bitcast.125) | data formatting | bytes 524288 | tf_op jit(solution)/shard_map/transpose | solution.py:396
  52.6 8.2 %shard_map.87 = (f32[4,2,2,2,128,128]{5,4,3,2,1,0:T(8,128)S(1)}, f32[2,2,2,128,128]{4,3,2,1,0:T(8,128)S(1)}, f32[2,2,2,128,128]{4,3,2,1,0:T(8,128)S(1)}, f32[2,2...) custom-call(s32[13]{0:T(128)S(1)} %concatenate.3.info.refs_0_, ...), custom_call_target="tpu_custom_call" | custom-call | tf_op jit(solution)/shard_map/pallas_call | solution.py:421
  65.8 3.4 %collective-permute-start.10 = (f32[2,2,128,128]{3,2,1,0:T(8,128)}, f32[2,2,128,128]{3,2,1,0:T(8,128)}, u32[]{:S(2)}, u32[]{:S(2)}) collective-permute-start(f32[2,2,128,128]{3,2,1,0:T(8,128)} %get-tuple-element.86), channel_id=1, source_target_pairs={{0,1},{1,0},{2,3},{3,2},{4,5},{5,4},{6,7},{7,6},{8,9},{9,8},{10,11... | collective-permute-start | bytes 786440 | tf_op jit(solution)/shard_map/ppermute | solution.py:30
  76.7 9.1 %collective-permute-start.15 = (f32[2,2,2,128,128]{4,3,2,1,0:T(8,128)S(1)}, f32[2,2,2,128,128]{4,3,2,1,0:T(8,128)S(1)}, u32[]{:S(2)}, u32[]{:S(2)}) collective-permute-start(f32[2,2,2,128,128]{4,3,2,1,0:T(8,128)S(1)} %pad_maximum_fusion.2.refs_6_), channel_id=1, source_target_pairs={{0,4},{4,0},{8,12},{12,8},{16,20},{20,16},{24,28},{28,24},{1,5},{5... | collective-permute-start | bytes 1572872 | tf_op jit(solution)/shard_map/ppermute | solution.py:30
  86.7 5.1 %collective-permute-start.4 = (f32[2,8,128]{2,1,0:T(8,128)S(1)}, f32[2,8,128]{2,1,0:T(8,128)S(1)}, u32[]{:S(2)}, u32[]{:S(2)}) collective-permute-start(f32[2,8,128]{2,1,0:T(8,128)S(1)} %get-tuple-element.28), channel_id=1, source_target_pairs={{0,4},{4,0},{8,12},{12,8},{16,20},{20,16},{24,28},{28,24},{1,5},{5... | collective-permute-start | bytes 24584 | tf_op jit(solution)/shard_map/ppermute | solution.py:41
  95.1 7.5 %collective-permute-done.5 = f32[2,8,128]{2,1,0:T(8,128)S(1)} collective-permute-done((f32[2,8,128]{2,1,0:T(8,128)S(1)}, f32[2,8,128]{2,1,0:T(8,128)S(1)}, u32[]{:S(2)}, u32[]{:S(2)}) %collective-permute-start.5) | collective-permute-done | bytes 8224 | tf_op jit(solution)/shard_map/ppermute | solution.py:41
  106.2 4.5 %collective-permute-start.7 = (f32[2,8,128]{2,1,0:T(8,128)S(1)}, f32[2,8,128]{2,1,0:T(8,128)S(1)}, u32[]{:S(2)}, u32[]{:S(2)}) collective-permute-start(f32[2,8,128]{2,1,0:T(8,128)S(1)} %add.144), channel_id=1, source_target_pairs={{0,1},{1,0},{2,3},{3,2},{4,5},{5,4},{6,7},{7,6},{8,9},{9,8},{10,11... | collective-permute-start | bytes 24584 | tf_op jit(solution)/shard_map/ppermute | solution.py:41
  113.6 3.3 %collective-permute-done.8 = f32[2,8,128]{2,1,0:T(8,128)S(1)} collective-permute-done((f32[2,8,128]{2,1,0:T(8,128)S(1)}, f32[2,8,128]{2,1,0:T(8,128)S(1)}, u32[]{:S(2)}, u32[]{:S(2)}) %collective-permute-start.8) | collective-permute-done | bytes 8224 | tf_op jit(solution)/shard_map/ppermute | solution.py:41
  116.9 7.4 %shard_map.88 = (f32[4,2,2,2,128,128]{5,4,3,2,1,0:T(8,128)S(1)}, f32[4,2,2,2,128,128]{5,4,3,2,1,0:T(8,128)S(1)}, f32[2,2,2,128,128]{4,3,2,1,0:T(8,128)S(1)}, f32...) custom-call(s32[13]{0:T(128)S(1)} %concatenate.3.info.refs_0_, ...), custom_call_target="tpu_custom_call" | custom-call | tf_op jit(solution)/shard_map/pallas_call | solution.py:421
  127.3 3.9 %collective-permute-start.26 = (f32[2,2,128,128]{3,2,1,0:T(8,128)S(1)}, f32[2,2,128,128]{3,2,1,0:T(8,128)S(1)}, u32[]{:S(2)}, u32[]{:S(2)}) collective-permute-start(f32[2,2,128,128]{3,2,1,0:T(8,128)S(1)} %get-tuple-element.74), channel_id=1, source_target_pairs={{0,1},{1,0},{2,3},{3,2},{4,5},{5,4},{6,7},{7,6},{8,9},{9,8},{10,11... | collective-permute-start | bytes 786440 | tf_op jit(solution)/shard_map/ppermute | solution.py:30
  131.9 3.8 %collective-permute-done.23 = f32[2,2,128,128]{3,2,1,0:T(8,128)S(1)} collective-permute-done((f32[2,2,128,128]{3,2,1,0:T(8,128)S(1)}, f32[2,2,128,128]{3,2,1,0:T(8,128)S(1)}, u32[]{:S(2)}, u32[]{:S(2)}) %collective-permute-start.23) | collective-permute-done | bytes 262176 | tf_op jit(solution)/shard_map/ppermute | solution.py:30
  135.8 4.8 %collective-permute-start.28 = (f32[2,2,2,128,128]{4,3,2,1,0:T(8,128)S(1)}, f32[2,2,2,128,128]{4,3,2,1,0:T(8,128)S(1)}, u32[]{:S(2)}, u32[]{:S(2)}) collective-permute-start(f32[2,2,2,128,128]{4,3,2,1,0:T(8,128)S(1)} %pad_maximum_fusion.4.refs_7_), channel_id=1, source_target_pairs={{0,4},{4,0},{8,12},{12,8},{16,20},{20,16},{24,28},{28,24},{1,5},{5... | collective-permute-start | bytes 1572872 | tf_op jit(solution)/shard_map/ppermute | solution.py:30
  141.5 8.8 %collective-permute-start.17 = (f32[2,8,128]{2,1,0:T(8,128)S(1)}, f32[2,8,128]{2,1,0:T(8,128)S(1)}, u32[]{:S(2)}, u32[]{:S(2)}) collective-permute-start(f32[2,8,128]{2,1,0:T(8,128)S(1)} %get-tuple-element.34), channel_id=1, source_target_pairs={{0,4},{4,0},{8,12},{12,8},{16,20},{20,16},{24,28},{28,24},{1,5},{5... | collective-permute-start | bytes 24584 | tf_op jit(solution)/shard_map/ppermute | solution.py:41
  151.9 10.9 %collective-permute-done.18 = f32[2,8,128]{2,1,0:T(8,128)S(1)} collective-permute-done((f32[2,8,128]{2,1,0:T(8,128)S(1)}, f32[2,8,128]{2,1,0:T(8,128)S(1)}, u32[]{:S(2)}, u32[]{:S(2)}) %collective-permute-start.18) | collective-permute-done | bytes 8224 | tf_op jit(solution)/shard_map/ppermute | solution.py:41
  162.8 3.6 %collective-permute-done.19 = f32[2,8,128]{2,1,0:T(8,128)S(1)} collective-permute-done((f32[2,8,128]{2,1,0:T(8,128)S(1)}, f32[2,8,128]{2,1,0:T(8,128)S(1)}, u32[]{:S(2)}, u32[]{:S(2)}) %collective-permute-start.19) | collective-permute-done | bytes 8224 | tf_op jit(solution)/shard_map/ppermute | solution.py:41
  166.5 4.1 %collective-permute-start.20 = (f32[2,8,128]{2,1,0:T(8,128)S(1)}, f32[2,8,128]{2,1,0:T(8,128)S(1)}, u32[]{:S(2)}, u32[]{:S(2)}) collective-permute-start(f32[2,8,128]{2,1,0:T(8,128)S(1)} %add.161), channel_id=1, source_target_pairs={{0,1},{1,0},{2,3},{3,2},{4,5},{5,4},{6,7},{7,6},{8,9},{9,8},{10,11... | collective-permute-start | bytes 24584 | tf_op jit(solution)/shard_map/ppermute | solution.py:41
  173.1 3.7 %collective-permute-done.21 = f32[2,8,128]{2,1,0:T(8,128)S(1)} collective-permute-done((f32[2,8,128]{2,1,0:T(8,128)S(1)}, f32[2,8,128]{2,1,0:T(8,128)S(1)}, u32[]{:S(2)}, u32[]{:S(2)}) %collective-permute-start.21) | collective-permute-done | bytes 8224 | tf_op jit(solution)/shard_map/ppermute | solution.py:41
  176.8 7.3 %shard_map.89 = (f32[4,2,2,2,128,128]{5,4,3,2,1,0:T(8,128)S(1)}, f32[4,2,2,2,128,128]{5,4,3,2,1,0:T(8,128)S(1)}, f32[2,2,2,128,128]{4,3,2,1,0:T(8,128)S(1)}, f32...) custom-call(s32[13]{0:T(128)S(1)} %concatenate.3.info.refs_0_, ...), custom_call_target="tpu_custom_call" | custom-call | tf_op jit(solution)/shard_map/pallas_call | solution.py:421
  189.4 8.9 %collective-permute-done.31 = f32[2,8,128]{2,1,0:T(8,128)S(1)} collective-permute-done((f32[2,8,128]{2,1,0:T(8,128)S(1)}, f32[2,8,128]{2,1,0:T(8,128)S(1)}, u32[]{:S(2)}, u32[]{:S(2)}) %collective-permute-start.31) | collective-permute-done | bytes 8224 | tf_op jit(solution)/shard_map/ppermute | solution.py:41
  198.3 3.6 %collective-permute-done.32 = f32[2,8,128]{2,1,0:T(8,128)S(1)} collective-permute-done((f32[2,8,128]{2,1,0:T(8,128)S(1)}, f32[2,8,128]{2,1,0:T(8,128)S(1)}, u32[]{:S(2)}, u32[]{:S(2)}) %collective-permute-start.32) | collective-permute-done | bytes 8224 | tf_op jit(solution)/shard_map/ppermute | solution.py:41
  205.6 4.6 %collective-permute-done.34 = f32[2,8,128]{2,1,0:T(8,128)S(1)} collective-permute-done((f32[2,8,128]{2,1,0:T(8,128)S(1)}, f32[2,8,128]{2,1,0:T(8,128)S(1)}, u32[]{:S(2)}, u32[]{:S(2)}) %collective-permute-start.34) | collective-permute-done | bytes 8224 | tf_op jit(solution)/shard_map/ppermute | solution.py:41
  (143 shorter events, 60.9 us)
Async XLA Ops:
  5.6 6.7 %collective-permute-start.1 = (f32[2,2,128,128]{3,2,1,0:T(8,128)S(1)}, f32[2,2,128,128]{3,2,1,0:T(8,128)S(1)}, u32[]{:S(2)}, u32[]{:S(2)}) collective-permute-start(f32[2,2,128,128]{3,2,1,0:T(8,128)S(1)} %get-tuple-element.27), channel_id=1, source_target_pairs={{1,2},{2,1},{5,6},{6,5},{9,10},{10,9},{13,14},{14,13},{17,18},{18,... | collective-permute-start | bytes 786440 | tf_op jit(solution)/shard_map/ppermute | solution.py:30
  6.3 12.0 %collective-permute-start = (f32[2,2,128,128]{3,2,1,0:T(8,128)S(1)}, f32[2,2,128,128]{3,2,1,0:T(8,128)S(1)}, u32[]{:S(2)}, u32[]{:S(2)}) collective-permute-start(f32[2,2,128,128]{3,2,1,0:T(8,128)S(1)} %get-tuple-element.26), channel_id=1, source_target_pairs={{0,1},{1,0},{2,3},{3,2},{4,5},{5,4},{6,7},{7,6},{8,9},{9,8},{10,11... | collective-permute-start | bytes 786440 | tf_op jit(solution)/shard_map/ppermute | solution.py:30
  18.4 31.4 %collective-permute-start.2 = (f32[2,2,2,128,128]{4,3,2,1,0:T(8,128)S(1)}, f32[2,2,2,128,128]{4,3,2,1,0:T(8,128)}, u32[]{:S(2)}, u32[]{:S(2)}) collective-permute-start(f32[2,2,2,128,128]{4,3,2,1,0:T(8,128)S(1)} %pad_maximum_fusion.refs_5_), channel_id=1, source_target_pairs={{0,4},{4,0},{8,12},{12,8},{16,20},{20,16},{24,28},{28,24},{1,5},{5... | collective-permute-start | bytes 1572872 | tf_op jit(solution)/shard_map/ppermute | solution.py:30
  18.5 31.3 %collective-permute-start.3 = (f32[2,2,2,128,128]{4,3,2,1,0:T(8,128)S(1)}, f32[2,2,2,128,128]{4,3,2,1,0:T(8,128)}, u32[]{:S(2)}, u32[]{:S(2)}) collective-permute-start(f32[2,2,2,128,128]{4,3,2,1,0:T(8,128)S(1)} %pad_maximum_fusion.1.refs_6_), channel_id=1, source_target_pairs={{4,8},{8,4},{12,16},{16,12},{20,24},{24,20},{5,9},{9,5},{13,17},{1... | collective-permute-start | bytes 1572872 | tf_op jit(solution)/shard_map/ppermute | solution.py:30
  63.0 7.6 %collective-permute-start.12 = (f32[2,2,2,128,128]{4,3,2,1,0:T(8,128)}, f32[2,2,2,128,128]{4,3,2,1,0:T(8,128)}, u32[]{:S(2)}, u32[]{:S(2)}) collective-permute-start(f32[2,2,2,128,128]{4,3,2,1,0:T(8,128)} %get-tuple-element.32), channel_id=1, source_target_pairs={{4,8},{8,4},{12,16},{16,12},{20,24},{24,20},{5,9},{9,5},{13,17},{1... | collective-permute-start | bytes 1572872 | tf_op jit(solution)/shard_map/ppermute | solution.py:30
  65.8 9.6 %collective-permute-start.10 = (f32[2,2,128,128]{3,2,1,0:T(8,128)}, f32[2,2,128,128]{3,2,1,0:T(8,128)}, u32[]{:S(2)}, u32[]{:S(2)}) collective-permute-start(f32[2,2,128,128]{3,2,1,0:T(8,128)} %get-tuple-element.86), channel_id=1, source_target_pairs={{0,1},{1,0},{2,3},{3,2},{4,5},{5,4},{6,7},{7,6},{8,9},{9,8},{10,11... | collective-permute-start | bytes 786440 | tf_op jit(solution)/shard_map/ppermute | solution.py:30
  69.2 6.2 %collective-permute-start.11 = (f32[2,2,128,128]{3,2,1,0:T(8,128)}, f32[2,2,128,128]{3,2,1,0:T(8,128)}, u32[]{:S(2)}, u32[]{:S(2)}) collective-permute-start(f32[2,2,128,128]{3,2,1,0:T(8,128)} %get-tuple-element.87), channel_id=1, source_target_pairs={{1,2},{2,1},{5,6},{6,5},{9,10},{10,9},{13,14},{14,13},{17,18},{18,... | collective-permute-start | bytes 786440 | tf_op jit(solution)/shard_map/ppermute | solution.py:30
  71.7 14.1 %collective-permute-start.13 = (f32[2,2,128,128]{3,2,1,0:T(8,128)S(1)}, f32[2,2,128,128]{3,2,1,0:T(8,128)S(1)}, u32[]{:S(2)}, u32[]{:S(2)}) collective-permute-start(f32[2,2,128,128]{3,2,1,0:T(8,128)S(1)} %get-tuple-element.82), channel_id=1, source_target_pairs={{0,1},{1,0},{2,3},{3,2},{4,5},{5,4},{6,7},{7,6},{8,9},{9,8},{10,11... | collective-permute-start | bytes 786440 | tf_op jit(solution)/shard_map/ppermute | solution.py:30
  72.8 13.0 %collective-permute-start.14 = (f32[2,2,128,128]{3,2,1,0:T(8,128)S(1)}, f32[2,2,128,128]{3,2,1,0:T(8,128)S(1)}, u32[]{:S(2)}, u32[]{:S(2)}) collective-permute-start(f32[2,2,128,128]{3,2,1,0:T(8,128)S(1)} %get-tuple-element.83), channel_id=1, source_target_pairs={{1,2},{2,1},{5,6},{6,5},{9,10},{10,9},{13,14},{14,13},{17,18},{18,... | collective-permute-start | bytes 786440 | tf_op jit(solution)/shard_map/ppermute | solution.py:30
  76.7 40.2 %collective-permute-start.15 = (f32[2,2,2,128,128]{4,3,2,1,0:T(8,128)S(1)}, f32[2,2,2,128,128]{4,3,2,1,0:T(8,128)S(1)}, u32[]{:S(2)}, u32[]{:S(2)}) collective-permute-start(f32[2,2,2,128,128]{4,3,2,1,0:T(8,128)S(1)} %pad_maximum_fusion.2.refs_6_), channel_id=1, source_target_pairs={{0,4},{4,0},{8,12},{12,8},{16,20},{20,16},{24,28},{28,24},{1,5},{5... | collective-permute-start | bytes 1572872 | tf_op jit(solution)/shard_map/ppermute | solution.py:30
  86.0 30.9 %collective-permute-start.16 = (f32[2,2,2,128,128]{4,3,2,1,0:T(8,128)S(1)}, f32[2,2,2,128,128]{4,3,2,1,0:T(8,128)S(1)}, u32[]{:S(2)}, u32[]{:S(2)}) collective-permute-start(f32[2,2,2,128,128]{4,3,2,1,0:T(8,128)S(1)} %pad_maximum_fusion.3.refs_7_), channel_id=1, source_target_pairs={{4,8},{8,4},{12,16},{16,12},{20,24},{24,20},{5,9},{9,5},{13,17},{1... | collective-permute-start | bytes 1572872 | tf_op jit(solution)/shard_map/ppermute | solution.py:30
  92.6 10.0 %collective-permute-start.5 = (f32[2,8,128]{2,1,0:T(8,128)S(1)}, f32[2,8,128]{2,1,0:T(8,128)S(1)}, u32[]{:S(2)}, u32[]{:S(2)}) collective-permute-start(f32[2,8,128]{2,1,0:T(8,128)S(1)} %add.142), channel_id=1, source_target_pairs={{0,8},{4,12},{8,0},{12,4},{16,24},{20,28},{24,16},{28,20},{1,9},{5... | collective-permute-start | bytes 24584 | tf_op jit(solution)/shard_map/ppermute | solution.py:41
  106.2 6.1 %collective-permute-start.7 = (f32[2,8,128]{2,1,0:T(8,128)S(1)}, f32[2,8,128]{2,1,0:T(8,128)S(1)}, u32[]{:S(2)}, u32[]{:S(2)}) collective-permute-start(f32[2,8,128]{2,1,0:T(8,128)S(1)} %add.144), channel_id=1, source_target_pairs={{0,1},{1,0},{2,3},{3,2},{4,5},{5,4},{6,7},{7,6},{8,9},{9,8},{10,11... | collective-permute-start | bytes 24584 | tf_op jit(solution)/shard_map/ppermute | solution.py:41
  126.4 9.2 %collective-permute-start.23 = (f32[2,2,128,128]{3,2,1,0:T(8,128)S(1)}, f32[2,2,128,128]{3,2,1,0:T(8,128)S(1)}, u32[]{:S(2)}, u32[]{:S(2)}) collective-permute-start(f32[2,2,128,128]{3,2,1,0:T(8,128)S(1)} %get-tuple-element.78), channel_id=1, source_target_pairs={{0,1},{1,0},{2,3},{3,2},{4,5},{5,4},{6,7},{7,6},{8,9},{9,8},{10,11... | collective-permute-start | bytes 786440 | tf_op jit(solution)/shard_map/ppermute | solution.py:30
  126.5 9.1 %collective-permute-start.24 = (f32[2,2,128,128]{3,2,1,0:T(8,128)S(1)}, f32[2,2,128,128]{3,2,1,0:T(8,128)S(1)}, u32[]{:S(2)}, u32[]{:S(2)}) collective-permute-start(f32[2,2,128,128]{3,2,1,0:T(8,128)S(1)} %get-tuple-element.79), channel_id=1, source_target_pairs={{1,2},{2,1},{5,6},{6,5},{9,10},{10,9},{13,14},{14,13},{17,18},{18,... | collective-permute-start | bytes 786440 | tf_op jit(solution)/shard_map/ppermute | solution.py:30
  127.3 13.3 %collective-permute-start.26 = (f32[2,2,128,128]{3,2,1,0:T(8,128)S(1)}, f32[2,2,128,128]{3,2,1,0:T(8,128)S(1)}, u32[]{:S(2)}, u32[]{:S(2)}) collective-permute-start(f32[2,2,128,128]{3,2,1,0:T(8,128)S(1)} %get-tuple-element.74), channel_id=1, source_target_pairs={{0,1},{1,0},{2,3},{3,2},{4,5},{5,4},{6,7},{7,6},{8,9},{9,8},{10,11... | collective-permute-start | bytes 786440 | tf_op jit(solution)/shard_map/ppermute | solution.py:30
  131.2 9.4 %collective-permute-start.27 = (f32[2,2,128,128]{3,2,1,0:T(8,128)S(1)}, f32[2,2,128,128]{3,2,1,0:T(8,128)S(1)}, u32[]{:S(2)}, u32[]{:S(2)}) collective-permute-start(f32[2,2,128,128]{3,2,1,0:T(8,128)S(1)} %get-tuple-element.75), channel_id=1, source_target_pairs={{1,2},{2,1},{5,6},{6,5},{9,10},{10,9},{13,14},{14,13},{17,18},{18,... | collective-permute-start | bytes 786440 | tf_op jit(solution)/shard_map/ppermute | solution.py:30
  135.8 41.0 %collective-permute-start.28 = (f32[2,2,2,128,128]{4,3,2,1,0:T(8,128)S(1)}, f32[2,2,2,128,128]{4,3,2,1,0:T(8,128)S(1)}, u32[]{:S(2)}, u32[]{:S(2)}) collective-permute-start(f32[2,2,2,128,128]{4,3,2,1,0:T(8,128)S(1)} %pad_maximum_fusion.4.refs_7_), channel_id=1, source_target_pairs={{0,4},{4,0},{8,12},{12,8},{16,20},{20,16},{24,28},{28,24},{1,5},{5... | collective-permute-start | bytes 1572872 | tf_op jit(solution)/shard_map/ppermute | solution.py:30
  140.8 35.9 %collective-permute-start.29 = (f32[2,2,2,128,128]{4,3,2,1,0:T(8,128)S(1)}, f32[2,2,2,128,128]{4,3,2,1,0:T(8,128)S(1)}, u32[]{:S(2)}, u32[]{:S(2)}) collective-permute-start(f32[2,2,2,128,128]{4,3,2,1,0:T(8,128)S(1)} %pad_maximum_fusion.5.refs_8_), channel_id=1, source_target_pairs={{4,8},{8,4},{12,16},{16,12},{20,24},{24,20},{5,9},{9,5},{13,17},{1... | collective-permute-start | bytes 1572872 | tf_op jit(solution)/shard_map/ppermute | solution.py:30
  141.5 9.6 %collective-permute-start.17 = (f32[2,8,128]{2,1,0:T(8,128)S(1)}, f32[2,8,128]{2,1,0:T(8,128)S(1)}, u32[]{:S(2)}, u32[]{:S(2)}) collective-permute-start(f32[2,8,128]{2,1,0:T(8,128)S(1)} %get-tuple-element.34), channel_id=1, source_target_pairs={{0,4},{4,0},{8,12},{12,8},{16,20},{20,16},{24,28},{28,24},{1,5},{5... | collective-permute-start | bytes 24584 | tf_op jit(solution)/shard_map/ppermute | solution.py:41
  151.1 11.7 %collective-permute-start.18 = (f32[2,8,128]{2,1,0:T(8,128)S(1)}, f32[2,8,128]{2,1,0:T(8,128)S(1)}, u32[]{:S(2)}, u32[]{:S(2)}) collective-permute-start(f32[2,8,128]{2,1,0:T(8,128)S(1)} %add.159), channel_id=1, source_target_pairs={{0,8},{4,12},{8,0},{12,4},{16,24},{20,28},{24,16},{28,20},{1,9},{5... | collective-permute-start | bytes 24584 | tf_op jit(solution)/shard_map/ppermute | solution.py:41
  184.0 26.2 %collective-permute-start.35 = (f32[2,2,2,128,128]{4,3,2,1,0:T(8,128)S(1)}, f32[2,2,2,128,128]{4,3,2,1,0:T(8,128)S(1)}, u32[]{:S(2)}, u32[]{:S(2)}) collective-permute-start(f32[2,2,2,128,128]{4,3,2,1,0:T(8,128)S(1)} %get-tuple-element.45), channel_id=1, source_target_pairs={{0,4},{4,0},{8,12},{12,8},{16,20},{20,16},{24,28},{28,24},{1,5},{5... | collective-permute-start | bytes 1572872 | tf_op jit(solution)/shard_map/ppermute | solution.py:30
  184.1 27.9 %collective-permute-start.36 = (f32[2,2,2,128,128]{4,3,2,1,0:T(8,128)S(1)}, f32[2,2,2,128,128]{4,3,2,1,0:T(8,128)S(1)}, u32[]{:S(2)}, u32[]{:S(2)}) collective-permute-start(f32[2,2,2,128,128]{4,3,2,1,0:T(8,128)S(1)} %get-tuple-element.47), channel_id=1, source_target_pairs={{4,8},{8,4},{12,16},{16,12},{20,24},{24,20},{5,9},{9,5},{13,17},{1... | collective-permute-start | bytes 1572872 | tf_op jit(solution)/shard_map/ppermute | solution.py:30
  187.4 10.9 %collective-permute-start.31 = (f32[2,8,128]{2,1,0:T(8,128)S(1)}, f32[2,8,128]{2,1,0:T(8,128)S(1)}, u32[]{:S(2)}, u32[]{:S(2)}) collective-permute-start(f32[2,8,128]{2,1,0:T(8,128)S(1)} %add.174), channel_id=1, source_target_pairs={{0,8},{4,12},{8,0},{12,4},{16,24},{20,28},{24,16},{28,20},{1,9},{5... | collective-permute-start | bytes 24584 | tf_op jit(solution)/shard_map/ppermute | solution.py:41
  (27 other events, 202.4 us)
where the time goes:
time: 222 us; the launch traced here: 220 us
  starting transfers between devices  76.5 us (34%)
  waiting for transfers between devices  72.9 us (33%)
  local copies, waits for them, and re-layouts  38.9 us (18%)
  Pallas kernels  26.3 us (12%)
  other arithmetic  3.32 us (1%)
    ppermute x15, waiting for transfers between devices, all_sum(): lax.ppermute(value, axis, [(i, i ^ step) for i in range(count)])  57.5 us
    ppermute x26, starting transfers between devices, swap(): return lax.ppermute(value, axis, pairs(axis, parity))  43.2 us
    ppermute x15, starting transfers between devices, all_sum(): lax.ppermute(value, axis, [(i, i ^ step) for i in range(count)])  33.3 us
    pallas_call x3, Pallas kernels, apply_op(): pl.pallas_call(functools.partial(apply_kernel, side, cap, stage), out_sha...  22.9 us
    reshape x2, local copies, waits for them, and re-layouts, local(): detector_weights.reshape(half, 2, half, 2).transpose(1, 0, 3, 2)  20 us
    ppermute x26, waiting for transfers between devices, swap(): return lax.ppermute(value, axis, pairs(axis, parity))  15.4 us
    transpose x1, local copies, waits for them, and re-layouts, local(): detector_weights.reshape(half, 2, half, 2).transpose(1, 0, 3, 2)  9.8 us
    unnamed x21, local copies, waits for them, and re-layouts  7.82 us
  transfers between devices with their start and end apart: 41, of which 22 were waited for; matrix products, arithmetic and copies ran while one was open for 16% of the time, Pallas kernels for 0%

commit v1 on v0

--- a/solution.py
+++ b/solution.py
@@ -30,19 +30,6 @@
     return lax.ppermute(value, axis, pairs(axis, parity))
 
 
-def all_sum(value):
-    for axis in ("row", "col"):
-        count = lax.axis_size(axis)
-        if count & (count - 1):
-            value = lax.psum(value, axis)
-            continue
-        step = 1
-        while step < count:
-            value = value + lax.ppermute(value, axis, [(i, i ^ step) for i in range(count)])
-            step *= 2
-    return value
-
-
 def split_np(mat):
     high = mat.astype(np.float32).astype(jnp.bfloat16)
     low = (mat - high.astype(np.float64)).astype(np.float32).astype(jnp.bfloat16)
@@ -52,7 +39,7 @@
 def tables(length):
     half = length // 2
     spot = np.arange(half)
-    lanes, rows = [], []
+    out = []
     for odd in (0, 1):
         phase = (spot[:, None] * (2 * spot[None, :] + odd)) % length
         angle = phase * (2.0 * math.pi / length)
@@ -60,11 +47,8 @@
         sin = np.sin(angle) / math.sqrt(length)
         forward = np.block([[cos, -sin], [sin, cos]])
         for mat in (forward, forward.T):
-            high, low = split_np(mat)
-            lanes.append(np.concatenate([high, high, low], axis=0))
-            high, low = split_np(mat.T)
-            rows.append(np.concatenate([high, low, high], axis=1))
-    return np.stack(lanes), np.stack(rows)
+            out.append(np.stack(split_np(mat)))
+    return np.stack(out)
 
 
 def split(value):
@@ -81,9 +65,13 @@
     return jnp.sum(ref, keepdims=True)
 
 
-def prep_kernel(side, cap, info, block, probe, zone_a, zone_b, rolled):
+def parities():
+    return lax.axis_index("row") % 2, lax.axis_index("col") % 2
+
+
+def zone_kernel(side, block, zone_a, zone_b):
     half = side // 2
-    par_r, par_c = info[0], info[1]
+    par_r, par_c = parities()
     for cz, out in ((0, zone_a), (1, zone_b)):
         right = (cz ^ 1 ^ par_c) == 1
         for rz in (0, 1):
@@ -92,17 +80,81 @@
                 rows = block[comp, pl.ds(base, half), :]
                 out[rz, comp] = jnp.where(right, rows[:, half:], rows[:, :half])
 
+
+def prep_kernel(side, cap, info, probe, weights, mats, rolled, sorted_weights, lanes, rows, held):
+    half = side // 2
+    for f in range(4):
+        high, low = mats[f, 0], mats[f, 1]
+        lanes[f, :side] = high
+        lanes[f, side : 2 * side] = high
+        lanes[f, 2 * side :] = low
+        other = f ^ 1
+        rows[other, :, :side] = high
+        rows[other, :, side : 2 * side] = low
+        rows[other, :, 2 * side :] = high
+
+    source = lax.broadcasted_iota(jnp.int32, (side, side), 0)
+    target = lax.broadcasted_iota(jnp.int32, (side, side), 1)
+    wanted = jnp.where(target < half, 2 * target, 2 * (target - half) + 1)
+    pick = jnp.where(source == wanted, 1.0, 0.0).astype(BF16)
+    value = weights[...]
+    first = value.astype(BF16)
+    rest = value - first.astype(F32)
+    second = rest.astype(BF16)
+    third = (rest - second.astype(F32)).astype(BF16)
+    moved = (dot(first, pick) + dot(second, pick)) + dot(third, pick)
+    for odd in (0, 1):
+        held[odd] = moved[:, odd * half : odd * half + half]
+    for which in (0, 1):
+        for odd in (0, 1):
+            to = slice(odd * half, odd * half + half)
+            sorted_weights[which, :, to] = held[odd, pl.ds(which, half, stride=2), :]
+
     for slot in range(cap):
-        row_by = lax.rem(info[5 + 2 * slot] + side, side)
-        col_by = lax.rem(info[6 + 2 * slot] + side, side)
+        row_by = lax.rem(info[1 + 2 * slot] + side, side)
+        col_by = lax.rem(info[2 + 2 * slot] + side, side)
         for comp in (0, 1):
-            moved = pltpu.roll(probe[comp], row_by, 0)
-            rolled[slot, comp] = pltpu.roll(moved, col_by, 1)
+            turned = pltpu.roll(probe[comp], row_by, 0)
+            rolled[slot, comp] = pltpu.roll(turned, col_by, 1)
+
+
+def reduce_kernel(own, got, sum_a, sum_b, out_a, out_b, sum_out):
+    for cz, out in ((0, out_a), (1, out_b)):
+        for b in range(4):
+            out[b // 2, b % 2] = own[cz, b // 2, b % 2] + got[cz, b // 2, b % 2]
+    sum_out[...] = sum_a[...] + sum_b[...]
+
+
+def has_partner(axis, zone):
+    at, count = lax.axis_index(axis), lax.axis_size(axis)
+    other = at + 1 - 2 * ((at % 2) ^ zone)
+    return jnp.logical_and(other >= 0, other < count)
+
+
+def merge_kernel(mine_a, mine_b, got_a, got_b, sum_a, sum_b, out, sum_out):
+    for cz, mine, got in ((0, mine_a, got_a), (1, mine_b, got_b)):
+        inside = has_partner("col", cz)
+        for comp in (0, 1):
+            out[cz, 0, comp] = mine[0, comp] + got[1, comp]
+            out[cz, 1, comp] = jnp.where(inside, mine[1, comp] + got[0, comp], 0.0)
+    sum_out[...] = sum_a[...] + sum_b[...]
+
+
+def first_kernel(zone_a, zone_b, got_a, got_b, out_a, out_b):
+    for cz, zone, got in ((0, zone_a, got_a), (1, zone_b, got_b)):
+        for rz, out in ((0, out_a), (1, out_b)):
+            for comp in (0, 1):
+                out[cz, 0, comp] = zone[rz, comp]
+                out[cz, 1, comp] = got[rz, comp]
+
+
+def add_kernel(sum_a, sum_b, sum_out):
+    sum_out[...] = sum_a[...] + sum_b[...]
 
 
 def coefficients(stage, sums):
-    norms = [total(s[0]) for s in sums]
-    prods = [total(s[1]) for s in sums]
+    norms = [total(a[0] + b[0]) for a, b in zip(sums[::2], sums[1::2])]
+    prods = [total(a[1] + b[1]) for a, b in zip(sums[::2], sums[1::2])]
     alphas, ratios = [], []
     for k in range(stage):
         if k == 0:
@@ -117,7 +169,7 @@
 
 def apply_kernel(side, cap, stage, *refs):
     half = side // 2
-    n_sums = stage
+    n_sums = 2 * stage
     info, rolled, weights, lanes, rows = refs[:5]
     pos = 5
     sums = refs[pos : pos + n_sums]
@@ -141,7 +193,8 @@
     pos += 5
     lhs, mid, rhs, freq, terms = refs[pos : pos + 5]
 
-    par_r, par_c, count = info[0], info[1], info[4]
+    par_r, par_c = parities()
+    count = info[0]
 
     if stage == 0:
         for z in range(4):
@@ -174,7 +227,7 @@
     def marks(slot):
         out = []
         for d in (0, 1):
-            off = info[5 + 2 * slot + d]
+            off = info[1 + 2 * slot + d]
             neg = off < 0
             out.append(jnp.where(neg, -1, 1))
             out.append(jnp.where(neg, 1 - (off + side), off))
@@ -340,14 +393,14 @@
 
 def final_kernel(side, stage, *refs):
     half = side // 2
-    info = refs[0]
-    sums = refs[1 : 1 + stage]
-    fields = refs[1 + stage : 1 + 2 * stage]
-    along_old = refs[1 + 2 * stage]
-    mine = refs[2 + 2 * stage : 6 + 2 * stage]
-    theirs = refs[6 + 2 * stage : 10 + 2 * stage]
-    solved, left = refs[10 + 2 * stage :]
-    par_r, par_c = info[0], info[1]
+    sums = refs[: 2 * stage]
+    refs = refs[2 * stage :]
+    fields = refs[:stage]
+    along_old = refs[stage]
+    mine = refs[stage + 1 : stage + 5]
+    theirs = refs[stage + 5 : stage + 9]
+    solved, left = refs[stage + 9 :]
+    par_r, par_c = parities()
     alphas, ratios = coefficients(stage, sums)
     for rz in (0, 1):
         for cz in (0, 1):
@@ -371,112 +424,142 @@
                             left[comp, at, right * half : right * half + half] = residual
 
 
+def call(kernel, outs, args, limit, scratch=()):
+    return pl.pallas_call(
+        kernel,
+        out_shape=tuple(outs),
+        in_specs=[SMEM if a.dtype == jnp.int32 else VMEM for a in args],
+        out_specs=tuple([VMEM] * len(outs)),
+        scratch_shapes=list(scratch),
+        compiler_params=pltpu.CompilerParams(vmem_limit_bytes=limit * 2**20),
+    )(*args)
+
+
+def stages():
+    out = []
+    for axis in ("row", "col"):
+        step = 1
+        while step < lax.axis_size(axis):
+            out.append((axis, step))
+            step *= 2
+    return out
+
+
+class Running:
+    def __init__(self, value):
+        self.value, self.left = value, stages()
+
+    def send(self):
+        if not self.left:
+            return jnp.zeros_like(self.value)
+        axis, step = self.left.pop(0)
+        count = lax.axis_size(axis)
+        return lax.ppermute(self.value, axis, [(i, i ^ step) for i in range(count)])
+
+    def finish(self):
+        got = self.send()
+        while self.left:
+            self.value = self.value + got
+            got = self.send()
+        return [self.value, got]
+
+
 def local(right_side, probe, detector_weights, offsets, counts):
     side = probe.shape[1]
     half = side // 2
     cap = offsets.shape[2]
-    row_at, col_at = lax.axis_index("row"), lax.axis_index("col")
-    row_n, col_n = lax.axis_size("row"), lax.axis_size("col")
-    par_r, par_c = row_at % 2, col_at % 2
-
-    def partner(at, par, count, zone):
-        other = at + (1 - 2 * (par ^ zone))
-        return jnp.logical_and(other >= 0, other < count)
-
-    near_col = [partner(col_at, par_c, col_n, z).astype(F32) for z in (0, 1)]
-    info = jnp.concatenate(
+    info = jnp.concatenate([counts.reshape(-1), offsets.reshape(-1)]).astype(jnp.int32)
+    mats = jnp.asarray(tables(side))
+
+    def shape(*dims, dtype=F32):
+        return jax.ShapeDtypeStruct(dims, dtype)
+
+    zone = shape(2, 2, half, half)
+    strip = shape(2, 2, 2, half, half)
+    whole = shape(4, 2, 2, 2, half, half)
+    tiny = shape(2, 8, half)
+
+    zones = call(functools.partial(zone_kernel, side), [zone, zone], [right_side], 4)
+    beyond = [swap(zones[z], "col", z) for z in (0, 1)]
+    rolled, weights, lanes, rows = call(
+        functools.partial(prep_kernel, side, cap),
         [
-            jnp.stack([par_r, par_c, par_r, par_c, counts[0, 0]]).astype(jnp.int32),
-            offsets.reshape(-1).astype(jnp.int32),
-        ]
+            shape(cap, 2, side, side),
+            shape(2, half, side),
+            shape(4, 3 * side, side, dtype=BF16),
+            shape(4, side, 3 * side, dtype=BF16),
+        ],
+        [info, probe, detector_weights, mats],
+        8,
+        [pltpu.VMEM((2, side, half), F32)],
     )
-    lanes, rows = tables(side)
-    lanes, rows = jnp.asarray(lanes), jnp.asarray(rows)
-    weights = (
-        detector_weights.reshape(half, 2, half, 2).transpose(1, 0, 3, 2).reshape(2, half, side)
-    )
-
-    zone = jax.ShapeDtypeStruct((2, 2, half, half), F32)
-    strip = jax.ShapeDtypeStruct((2, 2, 2, half, half), F32)
-    whole = jax.ShapeDtypeStruct((4, 2, 2, 2, half, half), F32)
-    tiny = jax.ShapeDtypeStruct((2, 8, half), F32)
-
-    zone_a, zone_b, rolled = pl.pallas_call(
-        functools.partial(prep_kernel, side, cap),
-        out_shape=(zone, zone, jax.ShapeDtypeStruct((cap, 2, side, side), F32)),
-        in_specs=[SMEM, VMEM, VMEM],
-        out_specs=(VMEM, VMEM, VMEM),
-        compiler_params=pltpu.CompilerParams(vmem_limit_bytes=16 * 2**20),
-    )(info, right_side, probe)
-
-    def apply_op(stage, sums, window, field_old, along_old):
-        args = [info, rolled, weights, lanes, rows, *sums, *window]
+    near = call(first_kernel, [strip, strip], [*zones, *beyond], 4)
+    far = [swap(near[z], "row", z) for z in (0, 1)]
+
+    sums, fields = [], []
+    field = along = None
+    for stage in range(ITERS):
+        args = [info, rolled, weights, lanes, rows, *sums, *near, *far]
         outs = [whole]
         if stage >= 1:
-            args.append(field_old)
+            args.append(field)
             outs.append(whole)
         if stage >= 2:
-            args.append(along_old)
-        outs += [strip] * 4 + [tiny]
-        got = pl.pallas_call(
+            args.append(along)
+        got = call(
             functools.partial(apply_kernel, side, cap, stage),
-            out_shape=tuple(outs),
-            in_specs=[SMEM] + [VMEM] * (len(args) - 1),
-            out_specs=tuple([VMEM] * len(outs)),
-            scratch_shapes=[
+            outs + [strip] * 4 + [tiny],
+            args,
+            16,
+            [
                 pltpu.VMEM((2, 2 * side, 3 * side), BF16),
                 pltpu.VMEM((2, 2 * side, side), F32),
                 pltpu.VMEM((2, 3 * side, 2 * side), BF16),
                 pltpu.VMEM((2, side, 2 * side), F32),
                 pltpu.VMEM((cap, 2, 2, 2, half, half), F32),
             ],
-            compiler_params=pltpu.CompilerParams(vmem_limit_bytes=32 * 2**20),
-        )(*args)
-        field = got[0]
-        along = got[1] if stage >= 1 else None
-        rest = got[2:] if stage >= 1 else got[1:]
-        return field, along, rest[0:2], rest[2:4], rest[4]
-
-    zones = (zone_a, zone_b)
-    beyond = [swap(zones[z], "col", z) for z in (0, 1)]
-    near = [
-        jnp.stack([jnp.stack([zones[cz][rz], beyond[cz][rz]]) for cz in (0, 1)]) for rz in (0, 1)
-    ]
-    far = [swap(near[z], "row", z) for z in (0, 1)]
-    window = (near[0], near[1], far[0], far[1])
-
-    sums, fields = [], []
-    field = along = None
-    for stage in range(ITERS):
-        field, along_new, own, sent, partial = apply_op(stage, sums, window, field, along)
+        )
+        field, along = got[0], got[1] if stage >= 1 else None
         fields.append(field)
-        along = along_new
-        reduced = [own[z] + swap(sent[z], "row", z) for z in (0, 1)]
-        sums = sums + [all_sum(partial)]
-        mine = [reduced[rz][cz] for rz in (0, 1) for cz in (0, 1)]
-        if stage + 1 < ITERS:
-            got = [swap(mine[2 * rz + cz], "col", cz) for rz in (0, 1) for cz in (0, 1)]
-            near = []
-            for rz in (0, 1):
-                parts = []
-                for cz in (0, 1):
-                    m, g = mine[2 * rz + cz], got[2 * rz + cz]
-                    parts.append(jnp.stack([m[0] + g[1], (m[1] + g[0]) * near_col[cz]]))
-                near.append(jnp.stack(parts))
-            far = [swap(near[z], "row", z) for z in (0, 1)]
-            window = (near[0], near[1], far[0], far[1])
+        own, sent, run = got[-5:-3], got[-3:-1], Running(got[-1])
+        last = stage + 1 == ITERS
+        from_b = swap(sent[1], "row", 1)
+        from_a = swap(sent[0], "row", 0)
+        part = shape(2, 2, half, half)
+        *mine_a, run.value = call(
+            reduce_kernel, [part, part, tiny], [own[0], from_a, run.value, run.send()], 4
+        )
+        if last:
+            got_a = [swap(mine_a[cz][1], "col", cz) for cz in (0, 1)]
+            (run.value,) = call(add_kernel, [tiny], [run.value, run.send()], 4)
         else:
-            got = [swap(mine[2 * rz + cz][1], "col", cz) for rz in (0, 1) for cz in (0, 1)]
-
-    out = jax.ShapeDtypeStruct(right_side.shape, F32)
-    args = [info, *sums, *fields, along, *mine, *got]
-    return pl.pallas_call(
+            got_a = [swap(mine_a[cz], "col", cz) for cz in (0, 1)]
+        *mine_b, run.value = call(
+            reduce_kernel, [part, part, tiny], [own[1], from_b, run.value, run.send()], 4
+        )
+        if last:
+            got_b = [swap(mine_b[cz][1], "col", cz) for cz in (0, 1)]
+            sums = sums + run.finish()
+            break
+        got_b = [swap(mine_b[cz], "col", cz) for cz in (0, 1)]
+        near_a, run.value = call(
+            merge_kernel, [strip, tiny], [*mine_a, *got_a, run.value, run.send()], 4
+        )
+        far_a = swap(near_a, "row", 0)
+        near_b, run.value = call(
+            merge_kernel, [strip, tiny], [*mine_b, *got_b, run.value, run.send()], 4
+        )
+        far_b = swap(near_b, "row", 1)
+        sums = sums + run.finish()
+        near, far = (near_a, near_b), (far_a, far_b)
+
+    out = shape(*right_side.shape)
+    return call(
         functools.partial(final_kernel, side, ITERS),
-        out_shape=(out, out),
-        in_specs=[SMEM] + [VMEM] * (len(args) - 1),
-        out_specs=(VMEM, VMEM),
-        compiler_params=pltpu.CompilerParams(vmem_limit_bytes=16 * 2**20),
-    )(*args)
+        [out, out],
+        [*sums, *fields, along, *mine_a, *mine_b, *got_a, *got_b],
+        8,
+    )
 
 
 def solution(mesh):

time: 222 us -> 170 us (0.77)
  local copies, waits for them, and re-layouts: 38.9 us -> 4.01 us
  waiting for transfers between devices: 72.9 us -> 43.9 us
  starting transfers between devices: 76.5 us -> 100 us
  Pallas kernels: 26.3 us -> 17.7 us
  other arithmetic: 3.32 us -> 0.08 us
    reshape x3 -> x1, local copies, waits for them, and re-layouts: 20.1 us -> 0.08 us  [local(): offsets.reshape(-1)]
    ppermute x15, waiting for transfers between devices: 57.5 us -> 38.2 us  [send(): return lax.ppermute(self.value, axis, [(i, i ^ step) for i in range(count)])]
    ppermute x26, starting transfers between devices: 43.2 us -> 61.1 us  [swap(): return lax.ppermute(value, axis, pairs(axis, parity))]
    transpose x1 -> x0, local copies, waits for them, and re-layouts: 9.8 us -> none  [local(): detector_weights.reshape(half, 2, half, 2).transpose(1, 0, 3, 2)]
    ppermute x26, waiting for transfers between devices: 15.4 us -> 5.7 us  [swap(): return lax.ppermute(value, axis, pairs(axis, parity))]
    pallas_call x5 -> x18, Pallas kernels: 26.3 us -> 17.7 us  [call(): pl.pallas_call(kernel, out_shape=tuple(outs), in_specs=[SMEM if a.dtype =...]
    ppermute x15, starting transfers between devices: 33.3 us -> 39.4 us  [send(): return lax.ppermute(self.value, axis, [(i, i ^ step) for i in range(count)])]
    unnamed x21 -> x9, local copies, waits for them, and re-layouts: 7.82 us -> 3.89 us
  transfers between devices with their start and end apart: 41 -> 41, of which waited for: 22 -> 15; matrix products, arithmetic and copies ran while one was open for 16% -> 1% of each run, Pallas kernels for 0% -> 1%
where the time goes in v1:
time: 170 us; the launch traced here: 168 us
  starting transfers between devices  100 us (59%)
  waiting for transfers between devices  43.9 us (26%)
  Pallas kernels  17.7 us (10%)
  local copies, waits for them, and re-layouts  4.01 us (2%)
    ppermute x26, starting transfers between devices, swap(): return lax.ppermute(value, axis, pairs(axis, parity))  61.1 us
    ppermute x15, starting transfers between devices, send(): return lax.ppermute(self.value, axis, [(i, i ^ step) for i in range(count)])  39.4 us
    ppermute x15, waiting for transfers between devices, send(): return lax.ppermute(self.value, axis, [(i, i ^ step) for i in range(count)])  38.2 us
    pallas_call x18, Pallas kernels, call(): pl.pallas_call(kernel, out_shape=tuple(outs), in_specs=[SMEM if a.dtype =...  17.7 us
    ppermute x26, waiting for transfers between devices, swap(): return lax.ppermute(value, axis, pairs(axis, parity))  5.7 us
    unnamed x9, local copies, waits for them, and re-layouts  3.89 us
  transfers between devices with their start and end apart: 41, of which 15 were waited for; matrix products, arithmetic and copies ran while one was open for 1% of the time, Pallas kernels for 1%

profile of v1, /device:TPU:0, one launch (start us, length us, event | category | flops | bytes accessed | tf_op | source)
XLA Modules:
  0.0 167.8 jit_solution(13771676022711570012)
XLA Ops:
  1.8 3.1 %collective-permute-start = (f32[2,2,128,128]{3,2,1,0:T(8,128)S(1)}, f32[2,2,128,128]{3,2,1,0:T(8,128)S(1)}, u32[]{:S(2)}, u32[]{:S(2)}) collective-permute-start(f32[2,2,128,128]{3,2,1,0:T(8,128)S(1)} %get-tuple-element.60.zone_a), channel_id=1, source_target_pairs={{0,1},{1,0},{2,3},{3,2},{4,5},{5,4},{6,7},{7,6},{8,9},{9,8},{10,11... | collective-permute-start | bytes 786440 | tf_op jit(solution)/shard_map/ppermute | solution.py:30
  5.6 5.6 %collective-permute-done.got_a = f32[2,2,128,128]{3,2,1,0:T(8,128)S(1)} collective-permute-done((f32[2,2,128,128]{3,2,1,0:T(8,128)S(1)}, f32[2,2,128,128]{3,2,1,0:T(8,128)S(1)}, u32[]{:S(2)}, u32[]{:S(2)}) %collective-permute-start) | collective-permute-done | bytes 262176 | tf_op jit(solution)/shard_map/ppermute | solution.py:30
  17.4 4.3 %shard_map.80 = (f32[4,2,2,2,128,128]{5,4,3,2,1,0:T(8,128)S(1)}, f32[2,2,2,128,128]{4,3,2,1,0:T(8,128)S(1)}, f32[2,2,2,128,128]{4,3,2,1,0:T(8,128)S(1)}, f32[2,2...) custom-call(s32[9]{0:T(128)S(1)} %pad_add_fusion.info.refs_0_, ...), custom_call_target="tpu_custom_call" | custom-call | tf_op jit(solution)/shard_map/pallas_call | solution.py:428
  21.7 10.2 %collective-permute-start.5 = (f32[2,2,2,128,128]{4,3,2,1,0:T(8,128)S(1)}, f32[2,2,2,128,128]{4,3,2,1,0:T(8,128)S(1)}, u32[]{:S(2)}, u32[]{:S(2)}) collective-permute-start(f32[2,2,2,128,128]{4,3,2,1,0:T(8,128)S(1)} %get-tuple-element.67), channel_id=1, source_target_pairs={{0,4},{4,0},{8,12},{12,8},{16,20},{20,16},{24,28},{28,24},{1,5},{5... | collective-permute-start | bytes 1572872 | tf_op jit(solution)/shard_map/ppermute | solution.py:30
  32.6 3.8 %collective-permute-start.6 = (f32[2,8,128]{2,1,0:T(8,128)S(1)}, f32[2,8,128]{2,1,0:T(8,128)S(1)}, u32[]{:S(2)}, u32[]{:S(2)}) collective-permute-start(f32[2,8,128]{2,1,0:T(8,128)S(1)} %get-tuple-element.68.sum_a), channel_id=1, source_target_pairs={{0,4},{4,0},{8,12},{12,8},{16,20},{20,16},{24,28},{28,24},{1,5},{5... | collective-permute-start | bytes 24584 | tf_op jit(solution)/shard_map/ppermute | solution.py:457
  39.2 4.6 %collective-permute-start.10 = (f32[2,2,128,128]{3,2,1,0:T(8,128)S(1)}, f32[2,2,128,128]{3,2,1,0:T(8,128)S(1)}, u32[]{:S(2)}, u32[]{:S(2)}) collective-permute-start(f32[2,2,128,128]{3,2,1,0:T(8,128)S(1)} %get-tuple-element.72.mine_a), channel_id=1, source_target_pairs={{0,1},{1,0},{2,3},{3,2},{4,5},{5,4},{6,7},{7,6},{8,9},{9,8},{10,11... | collective-permute-start | bytes 786440 | tf_op jit(solution)/shard_map/ppermute | solution.py:30
  44.5 3.5 %collective-permute-done.7.sum_b = f32[2,8,128]{2,1,0:T(8,128)S(1)} collective-permute-done((f32[2,8,128]{2,1,0:T(8,128)S(1)}, f32[2,8,128]{2,1,0:T(8,128)S(1)}, u32[]{:S(2)}, u32[]{:S(2)}) %collective-permute-start.7) | collective-permute-done | bytes 8224 | tf_op jit(solution)/shard_map/ppermute | solution.py:457
  48.0 4.6 %collective-permute-start.8 = (f32[2,2,128,128]{3,2,1,0:T(8,128)S(1)}, f32[2,2,128,128]{3,2,1,0:T(8,128)S(1)}, u32[]{:S(2)}, u32[]{:S(2)}) collective-permute-start(f32[2,2,128,128]{3,2,1,0:T(8,128)S(1)} %get-tuple-element.70.mine_a), channel_id=1, source_target_pairs={{0,1},{1,0},{2,3},{3,2},{4,5},{5,4},{6,7},{7,6},{8,9},{9,8},{10,11... | collective-permute-start | bytes 786440 | tf_op jit(solution)/shard_map/ppermute | solution.py:30
  57.7 5.6 %collective-permute-start.13 = (f32[2,8,128]{2,1,0:T(8,128)S(1)}, f32[2,8,128]{2,1,0:T(8,128)S(1)}, u32[]{:S(2)}, u32[]{:S(2)}) collective-permute-start(f32[2,8,128]{2,1,0:T(8,128)S(1)} %get-tuple-element.75.sum_a), channel_id=1, source_target_pairs={{0,1},{1,0},{2,3},{3,2},{4,5},{5,4},{6,7},{7,6},{8,9},{9,8},{10,11... | collective-permute-start | bytes 24584 | tf_op jit(solution)/shard_map/ppermute | solution.py:457
  70.4 4.6 %shard_map.85 = (f32[4,2,2,2,128,128]{5,4,3,2,1,0:T(8,128)S(1)}, f32[4,2,2,2,128,128]{5,4,3,2,1,0:T(8,128)S(1)}, f32[2,2,2,128,128]{4,3,2,1,0:T(8,128)S(1)}, f32...) custom-call(s32[9]{0:T(128)S(1)} %pad_add_fusion.info.refs_0_, ...), custom_call_target="tpu_custom_call" | custom-call | tf_op jit(solution)/shard_map/pallas_call | solution.py:428
  75.0 8.8 %collective-permute-start.18 = (f32[2,2,2,128,128]{4,3,2,1,0:T(8,128)S(1)}, f32[2,2,2,128,128]{4,3,2,1,0:T(8,128)S(1)}, u32[]{:S(2)}, u32[]{:S(2)}) collective-permute-start(f32[2,2,2,128,128]{4,3,2,1,0:T(8,128)S(1)} %get-tuple-element.83), channel_id=1, source_target_pairs={{0,4},{4,0},{8,12},{12,8},{16,20},{20,16},{24,28},{28,24},{1,5},{5... | collective-permute-start | bytes 1572872 | tf_op jit(solution)/shard_map/ppermute | solution.py:30
  84.4 2.9 %collective-permute-start.19 = (f32[2,8,128]{2,1,0:T(8,128)S(1)}, f32[2,8,128]{2,1,0:T(8,128)S(1)}, u32[]{:S(2)}, u32[]{:S(2)}) collective-permute-start(f32[2,8,128]{2,1,0:T(8,128)S(1)} %get-tuple-element.84.sum_a), channel_id=1, source_target_pairs={{0,4},{4,0},{8,12},{12,8},{16,20},{20,16},{24,28},{28,24},{1,5},{5... | collective-permute-start | bytes 24584 | tf_op jit(solution)/shard_map/ppermute | solution.py:457
  88.2 2.7 %collective-permute-start.20 = (f32[2,8,128]{2,1,0:T(8,128)S(1)}, f32[2,8,128]{2,1,0:T(8,128)S(1)}, u32[]{:S(2)}, u32[]{:S(2)}) collective-permute-start(f32[2,8,128]{2,1,0:T(8,128)S(1)} %get-tuple-element.85.sum_a), channel_id=1, source_target_pairs={{0,8},{4,12},{8,0},{12,4},{16,24},{20,28},{24,16},{28,20},{1,9},{5... | collective-permute-start | bytes 24584 | tf_op jit(solution)/shard_map/ppermute | solution.py:457
  92.7 5.7 %collective-permute-done.20.sum_b = f32[2,8,128]{2,1,0:T(8,128)S(1)} collective-permute-done((f32[2,8,128]{2,1,0:T(8,128)S(1)}, f32[2,8,128]{2,1,0:T(8,128)S(1)}, u32[]{:S(2)}, u32[]{:S(2)}) %collective-permute-start.20) | collective-permute-done | bytes 8224 | tf_op jit(solution)/shard_map/ppermute | solution.py:457
  98.4 2.9 %collective-permute-start.21 = (f32[2,2,128,128]{3,2,1,0:T(8,128)S(1)}, f32[2,2,128,128]{3,2,1,0:T(8,128)S(1)}, u32[]{:S(2)}, u32[]{:S(2)}) collective-permute-start(f32[2,2,128,128]{3,2,1,0:T(8,128)S(1)} %get-tuple-element.86.mine_a), channel_id=1, source_target_pairs={{0,1},{1,0},{2,3},{3,2},{4,5},{5,4},{6,7},{7,6},{8,9},{9,8},{10,11... | collective-permute-start | bytes 786440 | tf_op jit(solution)/shard_map/ppermute | solution.py:30
  106.1 4.7 %collective-permute-start.26 = (f32[2,8,128]{2,1,0:T(8,128)S(1)}, f32[2,8,128]{2,1,0:T(8,128)S(1)}, u32[]{:S(2)}, u32[]{:S(2)}) collective-permute-start(f32[2,8,128]{2,1,0:T(8,128)S(1)} %get-tuple-element.91.sum_a), channel_id=1, source_target_pairs={{0,1},{1,0},{2,3},{3,2},{4,5},{5,4},{6,7},{7,6},{8,9},{9,8},{10,11... | collective-permute-start | bytes 24584 | tf_op jit(solution)/shard_map/ppermute | solution.py:457
  118.1 4.8 %shard_map.90 = (f32[4,2,2,2,128,128]{5,4,3,2,1,0:T(8,128)S(1)}, f32[4,2,2,2,128,128]{5,4,3,2,1,0:T(8,128)S(1)}, f32[2,2,2,128,128]{4,3,2,1,0:T(8,128)S(1)}, f32...) custom-call(s32[9]{0:T(128)S(1)} %pad_add_fusion.info.refs_0_, ...), custom_call_target="tpu_custom_call" | custom-call | tf_op jit(solution)/shard_map/pallas_call | solution.py:428
  122.8 8.6 %collective-permute-start.31 = (f32[2,2,2,128,128]{4,3,2,1,0:T(8,128)S(1)}, f32[2,2,2,128,128]{4,3,2,1,0:T(8,128)S(1)}, u32[]{:S(2)}, u32[]{:S(2)}) collective-permute-start(f32[2,2,2,128,128]{4,3,2,1,0:T(8,128)S(1)} %get-tuple-element.100), channel_id=1, source_target_pairs={{0,4},{4,0},{8,12},{12,8},{16,20},{20,16},{24,28},{28,24},{1,5},{5... | collective-permute-start | bytes 1572872 | tf_op jit(solution)/shard_map/ppermute | solution.py:30
  132.1 3.8 %collective-permute-start.32 = (f32[2,8,128]{2,1,0:T(8,128)S(1)}, f32[2,8,128]{2,1,0:T(8,128)S(1)}, u32[]{:S(2)}, u32[]{:S(2)}) collective-permute-start(f32[2,8,128]{2,1,0:T(8,128)S(1)} %get-tuple-element.101.sum_a), channel_id=1, source_target_pairs={{0,4},{4,0},{8,12},{12,8},{16,20},{20,16},{24,28},{28,24},{1,5},{5... | collective-permute-start | bytes 24584 | tf_op jit(solution)/shard_map/ppermute | solution.py:457
  139.1 7.9 %collective-permute-done.33.sum_b = f32[2,8,128]{2,1,0:T(8,128)S(1)} collective-permute-done((f32[2,8,128]{2,1,0:T(8,128)S(1)}, f32[2,8,128]{2,1,0:T(8,128)S(1)}, u32[]{:S(2)}, u32[]{:S(2)}) %collective-permute-start.33) | collective-permute-done | bytes 8224 | tf_op jit(solution)/shard_map/ppermute | solution.py:457
  149.0 5.2 %collective-permute-start.37 = (f32[2,128,128]{2,1,0:T(8,128)S(1)}, f32[2,128,128]{2,1,0:T(8,128)S(1)}, u32[]{:S(2)}, u32[]{:S(2)}) collective-permute-start(f32[2,128,128]{2,1,0:T(8,128)S(1)} %slice_bitcast_fusion.3), channel_id=1, source_target_pairs={{0,1},{1,0},{2,3},{3,2},{4,5},{5,4},{6,7},{7,6},{8,9},{9,8},{10,11... | collective-permute-start | bytes 393224 | tf_op jit(solution)/shard_map/ppermute | solution.py:30
  155.0 2.9 %collective-permute-start.39 = (f32[2,128,128]{2,1,0:T(8,128)S(1)}, f32[2,128,128]{2,1,0:T(8,128)S(1)}, u32[]{:S(2)}, u32[]{:S(2)}) collective-permute-start(f32[2,128,128]{2,1,0:T(8,128)S(1)} %slice_bitcast_fusion.1), channel_id=1, source_target_pairs={{0,1},{1,0},{2,3},{3,2},{4,5},{5,4},{6,7},{7,6},{8,9},{9,8},{10,11... | collective-permute-start | bytes 393224 | tf_op jit(solution)/shard_map/ppermute | solution.py:30
  158.0 3.6 %collective-permute-done.35 = f32[2,8,128]{2,1,0:T(8,128)S(1)} collective-permute-done((f32[2,8,128]{2,1,0:T(8,128)S(1)}, f32[2,8,128]{2,1,0:T(8,128)S(1)}, u32[]{:S(2)}, u32[]{:S(2)}) %collective-permute-start.35) | collective-permute-done | bytes 8224 | tf_op jit(solution)/shard_map/ppermute | solution.py:457
  162.8 3.3 %collective-permute-done.36.refs_5_ = f32[2,8,128]{2,1,0:T(8,128)S(1)} collective-permute-done((f32[2,8,128]{2,1,0:T(8,128)S(1)}, f32[2,8,128]{2,1,0:T(8,128)S(1)}, u32[]{:S(2)}, u32[]{:S(2)}) %collective-permute-start.36) | collective-permute-done | bytes 8224 | tf_op jit(solution)/shard_map/ppermute | solution.py:457
  (92 shorter events, 48.5 us)
Async XLA Ops:
  1.8 9.4 %collective-permute-start = (f32[2,2,128,128]{3,2,1,0:T(8,128)S(1)}, f32[2,2,128,128]{3,2,1,0:T(8,128)S(1)}, u32[]{:S(2)}, u32[]{:S(2)}) collective-permute-start(f32[2,2,128,128]{3,2,1,0:T(8,128)S(1)} %get-tuple-element.60.zone_a), channel_id=1, source_target_pairs={{0,1},{1,0},{2,3},{3,2},{4,5},{5,4},{6,7},{7,6},{8,9},{9,8},{10,11... | collective-permute-start | bytes 786440 | tf_op jit(solution)/shard_map/ppermute | solution.py:30
  21.7 15.5 %collective-permute-start.5 = (f32[2,2,2,128,128]{4,3,2,1,0:T(8,128)S(1)}, f32[2,2,2,128,128]{4,3,2,1,0:T(8,128)S(1)}, u32[]{:S(2)}, u32[]{:S(2)}) collective-permute-start(f32[2,2,2,128,128]{4,3,2,1,0:T(8,128)S(1)} %get-tuple-element.67), channel_id=1, source_target_pairs={{0,4},{4,0},{8,12},{12,8},{16,20},{20,16},{24,28},{28,24},{1,5},{5... | collective-permute-start | bytes 1572872 | tf_op jit(solution)/shard_map/ppermute | solution.py:30
  31.9 12.5 %collective-permute-start.4 = (f32[2,2,2,128,128]{4,3,2,1,0:T(8,128)S(1)}, f32[2,2,2,128,128]{4,3,2,1,0:T(8,128)S(1)}, u32[]{:S(2)}, u32[]{:S(2)}) collective-permute-start(f32[2,2,2,128,128]{4,3,2,1,0:T(8,128)S(1)} %get-tuple-element.65), channel_id=1, source_target_pairs={{4,8},{8,4},{12,16},{16,12},{20,24},{24,20},{5,9},{9,5},{13,17},{1... | collective-permute-start | bytes 1572872 | tf_op jit(solution)/shard_map/ppermute | solution.py:30
  37.3 10.6 %collective-permute-start.7 = (f32[2,8,128]{2,1,0:T(8,128)S(1)}, f32[2,8,128]{2,1,0:T(8,128)S(1)}, u32[]{:S(2)}, u32[]{:S(2)}) collective-permute-start(f32[2,8,128]{2,1,0:T(8,128)S(1)} %get-tuple-element.69.sum_a), channel_id=1, source_target_pairs={{0,8},{4,12},{8,0},{12,4},{16,24},{20,28},{24,16},{28,20},{1,9},{5... | collective-permute-start | bytes 24584 | tf_op jit(solution)/shard_map/ppermute | solution.py:457
  39.2 18.5 %collective-permute-start.10 = (f32[2,2,128,128]{3,2,1,0:T(8,128)S(1)}, f32[2,2,128,128]{3,2,1,0:T(8,128)S(1)}, u32[]{:S(2)}, u32[]{:S(2)}) collective-permute-start(f32[2,2,128,128]{3,2,1,0:T(8,128)S(1)} %get-tuple-element.72.mine_a), channel_id=1, source_target_pairs={{0,1},{1,0},{2,3},{3,2},{4,5},{5,4},{6,7},{7,6},{8,9},{9,8},{10,11... | collective-permute-start | bytes 786440 | tf_op jit(solution)/shard_map/ppermute | solution.py:30
  43.8 13.9 %collective-permute-start.11 = (f32[2,2,128,128]{3,2,1,0:T(8,128)S(1)}, f32[2,2,128,128]{3,2,1,0:T(8,128)S(1)}, u32[]{:S(2)}, u32[]{:S(2)}) collective-permute-start(f32[2,2,128,128]{3,2,1,0:T(8,128)S(1)} %get-tuple-element.73.mine_b), channel_id=1, source_target_pairs={{1,2},{2,1},{5,6},{6,5},{9,10},{10,9},{13,14},{14,13},{17,18},{18,... | collective-permute-start | bytes 786440 | tf_op jit(solution)/shard_map/ppermute | solution.py:30
  48.0 15.4 %collective-permute-start.8 = (f32[2,2,128,128]{3,2,1,0:T(8,128)S(1)}, f32[2,2,128,128]{3,2,1,0:T(8,128)S(1)}, u32[]{:S(2)}, u32[]{:S(2)}) collective-permute-start(f32[2,2,128,128]{3,2,1,0:T(8,128)S(1)} %get-tuple-element.70.mine_a), channel_id=1, source_target_pairs={{0,1},{1,0},{2,3},{3,2},{4,5},{5,4},{6,7},{7,6},{8,9},{9,8},{10,11... | collective-permute-start | bytes 786440 | tf_op jit(solution)/shard_map/ppermute | solution.py:30
  52.6 10.7 %collective-permute-start.9 = (f32[2,2,128,128]{3,2,1,0:T(8,128)S(1)}, f32[2,2,128,128]{3,2,1,0:T(8,128)S(1)}, u32[]{:S(2)}, u32[]{:S(2)}) collective-permute-start(f32[2,2,128,128]{3,2,1,0:T(8,128)S(1)} %get-tuple-element.71.mine_b), channel_id=1, source_target_pairs={{1,2},{2,1},{5,6},{6,5},{9,10},{10,9},{13,14},{14,13},{17,18},{18,... | collective-permute-start | bytes 786440 | tf_op jit(solution)/shard_map/ppermute | solution.py:30
  57.7 7.3 %collective-permute-start.13 = (f32[2,8,128]{2,1,0:T(8,128)S(1)}, f32[2,8,128]{2,1,0:T(8,128)S(1)}, u32[]{:S(2)}, u32[]{:S(2)}) collective-permute-start(f32[2,8,128]{2,1,0:T(8,128)S(1)} %get-tuple-element.75.sum_a), channel_id=1, source_target_pairs={{0,1},{1,0},{2,3},{3,2},{4,5},{5,4},{6,7},{7,6},{8,9},{9,8},{10,11... | collective-permute-start | bytes 24584 | tf_op jit(solution)/shard_map/ppermute | solution.py:457
  75.0 13.2 %collective-permute-start.18 = (f32[2,2,2,128,128]{4,3,2,1,0:T(8,128)S(1)}, f32[2,2,2,128,128]{4,3,2,1,0:T(8,128)S(1)}, u32[]{:S(2)}, u32[]{:S(2)}) collective-permute-start(f32[2,2,2,128,128]{4,3,2,1,0:T(8,128)S(1)} %get-tuple-element.83), channel_id=1, source_target_pairs={{0,4},{4,0},{8,12},{12,8},{16,20},{20,16},{24,28},{28,24},{1,5},{5... | collective-permute-start | bytes 1572872 | tf_op jit(solution)/shard_map/ppermute | solution.py:30
  83.7 8.9 %collective-permute-start.17 = (f32[2,2,2,128,128]{4,3,2,1,0:T(8,128)S(1)}, f32[2,2,2,128,128]{4,3,2,1,0:T(8,128)S(1)}, u32[]{:S(2)}, u32[]{:S(2)}) collective-permute-start(f32[2,2,2,128,128]{4,3,2,1,0:T(8,128)S(1)} %get-tuple-element.81), channel_id=1, source_target_pairs={{4,8},{8,4},{12,16},{16,12},{20,24},{24,20},{5,9},{9,5},{13,17},{1... | collective-permute-start | bytes 1572872 | tf_op jit(solution)/shard_map/ppermute | solution.py:30
  88.2 10.1 %collective-permute-start.20 = (f32[2,8,128]{2,1,0:T(8,128)S(1)}, f32[2,8,128]{2,1,0:T(8,128)S(1)}, u32[]{:S(2)}, u32[]{:S(2)}) collective-permute-start(f32[2,8,128]{2,1,0:T(8,128)S(1)} %get-tuple-element.85.sum_a), channel_id=1, source_target_pairs={{0,8},{4,12},{8,0},{12,4},{16,24},{20,28},{24,16},{28,20},{1,9},{5... | collective-permute-start | bytes 24584 | tf_op jit(solution)/shard_map/ppermute | solution.py:457
  90.9 15.1 %collective-permute-start.23 = (f32[2,2,128,128]{3,2,1,0:T(8,128)S(1)}, f32[2,2,128,128]{3,2,1,0:T(8,128)S(1)}, u32[]{:S(2)}, u32[]{:S(2)}) collective-permute-start(f32[2,2,128,128]{3,2,1,0:T(8,128)S(1)} %get-tuple-element.88.mine_a), channel_id=1, source_target_pairs={{0,1},{1,0},{2,3},{3,2},{4,5},{5,4},{6,7},{7,6},{8,9},{9,8},{10,11... | collective-permute-start | bytes 786440 | tf_op jit(solution)/shard_map/ppermute | solution.py:30
  92.0 14.1 %collective-permute-start.24 = (f32[2,2,128,128]{3,2,1,0:T(8,128)S(1)}, f32[2,2,128,128]{3,2,1,0:T(8,128)S(1)}, u32[]{:S(2)}, u32[]{:S(2)}) collective-permute-start(f32[2,2,128,128]{3,2,1,0:T(8,128)S(1)} %get-tuple-element.89.mine_b), channel_id=1, source_target_pairs={{1,2},{2,1},{5,6},{6,5},{9,10},{10,9},{13,14},{14,13},{17,18},{18,... | collective-permute-start | bytes 786440 | tf_op jit(solution)/shard_map/ppermute | solution.py:30
  98.4 12.5 %collective-permute-start.21 = (f32[2,2,128,128]{3,2,1,0:T(8,128)S(1)}, f32[2,2,128,128]{3,2,1,0:T(8,128)S(1)}, u32[]{:S(2)}, u32[]{:S(2)}) collective-permute-start(f32[2,2,128,128]{3,2,1,0:T(8,128)S(1)} %get-tuple-element.86.mine_a), channel_id=1, source_target_pairs={{0,1},{1,0},{2,3},{3,2},{4,5},{5,4},{6,7},{7,6},{8,9},{9,8},{10,11... | collective-permute-start | bytes 786440 | tf_op jit(solution)/shard_map/ppermute | solution.py:30
  101.3 9.6 %collective-permute-start.22 = (f32[2,2,128,128]{3,2,1,0:T(8,128)S(1)}, f32[2,2,128,128]{3,2,1,0:T(8,128)S(1)}, u32[]{:S(2)}, u32[]{:S(2)}) collective-permute-start(f32[2,2,128,128]{3,2,1,0:T(8,128)S(1)} %get-tuple-element.87.mine_b), channel_id=1, source_target_pairs={{1,2},{2,1},{5,6},{6,5},{9,10},{10,9},{13,14},{14,13},{17,18},{18,... | collective-permute-start | bytes 786440 | tf_op jit(solution)/shard_map/ppermute | solution.py:30
  122.8 13.9 %collective-permute-start.31 = (f32[2,2,2,128,128]{4,3,2,1,0:T(8,128)S(1)}, f32[2,2,2,128,128]{4,3,2,1,0:T(8,128)S(1)}, u32[]{:S(2)}, u32[]{:S(2)}) collective-permute-start(f32[2,2,2,128,128]{4,3,2,1,0:T(8,128)S(1)} %get-tuple-element.100), channel_id=1, source_target_pairs={{0,4},{4,0},{8,12},{12,8},{16,20},{20,16},{24,28},{28,24},{1,5},{5... | collective-permute-start | bytes 1572872 | tf_op jit(solution)/shard_map/ppermute | solution.py:30
  131.4 22.8 %collective-permute-start.30 = (f32[2,2,2,128,128]{4,3,2,1,0:T(8,128)S(1)}, f32[2,2,2,128,128]{4,3,2,1,0:T(8,128)S(1)}, u32[]{:S(2)}, u32[]{:S(2)}) collective-permute-start(f32[2,2,2,128,128]{4,3,2,1,0:T(8,128)S(1)} %get-tuple-element.98), channel_id=1, source_target_pairs={{4,8},{8,4},{12,16},{16,12},{20,24},{24,20},{5,9},{9,5},{13,17},{1... | collective-permute-start | bytes 1572872 | tf_op jit(solution)/shard_map/ppermute | solution.py:30
  136.8 10.2 %collective-permute-start.33 = (f32[2,8,128]{2,1,0:T(8,128)S(1)}, f32[2,8,128]{2,1,0:T(8,128)S(1)}, u32[]{:S(2)}, u32[]{:S(2)}) collective-permute-start(f32[2,8,128]{2,1,0:T(8,128)S(1)} %get-tuple-element.102.sum_a), channel_id=1, source_target_pairs={{0,8},{4,12},{8,0},{12,4},{16,24},{20,28},{24,16},{28,20},{1,9},{5... | collective-permute-start | bytes 24584 | tf_op jit(solution)/shard_map/ppermute | solution.py:457
  147.0 7.2 %collective-permute-start.34 = (f32[2,8,128]{2,1,0:T(8,128)S(1)}, f32[2,8,128]{2,1,0:T(8,128)S(1)}, u32[]{:S(2)}, u32[]{:S(2)}) collective-permute-start(f32[2,8,128]{2,1,0:T(8,128)S(1)} %shard_map.92.sum_a), channel_id=1, source_target_pairs={{0,16},{4,20},{8,24},{12,28},{16,0},{20,4},{24,8},{28,12},{1,17},{... | collective-permute-start | bytes 24584 | tf_op jit(solution)/shard_map/ppermute | solution.py:457
  148.3 17.8 %collective-permute-start.38 = (f32[2,128,128]{2,1,0:T(8,128)S(1)}, f32[2,128,128]{2,1,0:T(8,128)S(1)}, u32[]{:S(2)}, u32[]{:S(2)}) collective-permute-start(f32[2,128,128]{2,1,0:T(8,128)S(1)} %slice_bitcast_fusion.2), channel_id=1, source_target_pairs={{1,2},{2,1},{5,6},{6,5},{9,10},{10,9},{13,14},{14,13},{17,18},{18,... | collective-permute-start | bytes 393224 | tf_op jit(solution)/shard_map/ppermute | solution.py:30
  149.0 17.1 %collective-permute-start.37 = (f32[2,128,128]{2,1,0:T(8,128)S(1)}, f32[2,128,128]{2,1,0:T(8,128)S(1)}, u32[]{:S(2)}, u32[]{:S(2)}) collective-permute-start(f32[2,128,128]{2,1,0:T(8,128)S(1)} %slice_bitcast_fusion.3), channel_id=1, source_target_pairs={{0,1},{1,0},{2,3},{3,2},{4,5},{5,4},{6,7},{7,6},{8,9},{9,8},{10,11... | collective-permute-start | bytes 393224 | tf_op jit(solution)/shard_map/ppermute | solution.py:30
  154.3 11.8 %collective-permute-start.40 = (f32[2,128,128]{2,1,0:T(8,128)S(1)}, f32[2,128,128]{2,1,0:T(8,128)S(1)}, u32[]{:S(2)}, u32[]{:S(2)}) collective-permute-start(f32[2,128,128]{2,1,0:T(8,128)S(1)} %slice_bitcast_fusion), channel_id=1, source_target_pairs={{1,2},{2,1},{5,6},{6,5},{9,10},{10,9},{13,14},{14,13},{17,18},{18,... | collective-permute-start | bytes 393224 | tf_op jit(solution)/shard_map/ppermute | solution.py:30
  155.0 11.2 %collective-permute-start.39 = (f32[2,128,128]{2,1,0:T(8,128)S(1)}, f32[2,128,128]{2,1,0:T(8,128)S(1)}, u32[]{:S(2)}, u32[]{:S(2)}) collective-permute-start(f32[2,128,128]{2,1,0:T(8,128)S(1)} %slice_bitcast_fusion.1), channel_id=1, source_target_pairs={{0,1},{1,0},{2,3},{3,2},{4,5},{5,4},{6,7},{7,6},{8,9},{9,8},{10,11... | collective-permute-start | bytes 393224 | tf_op jit(solution)/shard_map/ppermute | solution.py:30
  (21 other events, 104.7 us)
